TPU v7x, 512 devices: a whole 4x8x8 slice. The times are simulated.
512 devices in a mesh: row: 32 (over z_hi, x, core), col: 16 (over y, z_lo).
Axes of the slice: x: 4, y: 8, z: 8 (z_hi: 4, z_lo: 2; z = z_hi * 2 + z_lo), core: 2. Of those that a mesh axis runs over, the one named last changes fastest.
Arguments:
- kernel: bfloat16 [20480, 20480], P('row', 'col'), as said below
- labels: int32 [20480], P('row'), may hold values from -1 to 1, as said below
- start_dual: float32 [20480, 128], P('row'), may hold values from 0 to 1
- penalty: float32 [128], replicated, may hold values from 2 to 6
- box: float32 [128], replicated, may hold values from 0.1 to 1
Outputs:
- dual: float32 [20480, 128], P(('row', 'col'))
- scaled_mult: float32 [20480, 128], P(('row', 'col'))
- gaps: float32 [3, 128], replicated
- offset: float32 [128], replicated
Inputs may be any that keep to these rules, and one draw needn't show every extreme that they name: `labels`: each entry is -1 or +1. `kernel`: a symmetric matrix.
All inputs are finite; a program needn't handle non-finite values.
Results may differ from a plain program's by a relative error of at most 0.0027.
Values may be sent and summed in bfloat16 or wider, within the bound.
A program may use at most 64 MiB of HBM per device.

v0:
```python
import functools

import jax
import jax.numpy as jnp
from jax import lax
from jax.sharding import Mesh
from jax.sharding import PartitionSpec as P

ITERS = 3
ROW = ("row_0", "row_1", "row_2")
COL = ("col_0", "col_1")
ROW_COL = ("row_0", "row_1", "row_2", "col_0", "col_1")


def broadcast(value, axis, root):
    return lax.dynamic_index_in_dim(lax.all_gather(value, axis), root, 0, keepdims=False)


def from_everyone(value, axis):
    length = lax.axis_size(axis)
    return lax.all_to_all(
        jnp.broadcast_to(value[None], (length, *value.shape)), axis, 0, 0, tiled=True
    )


def in_order(tiles, dim):
    tiles = jnp.moveaxis(tiles, 0, dim)
    lengths = tiles.shape
    return tiles.reshape(*lengths[:dim], lengths[dim] * lengths[dim + 1], *lengths[dim + 2 :])


def collect(value, axis, dim):
    tiles = from_everyone(value, axis)
    return in_order(tiles, dim)


def cut_along(value, dim, length):
    before, after = (value.shape[:dim], value.shape[dim + 1 :])
    return jnp.moveaxis(value.reshape(*before, length, -1, *after), dim, 0)


def sent_and_summed(value, axis, dim):
    length = lax.axis_size(axis)
    tiles = lax.all_to_all(cut_along(value, dim, length), axis, 0, 0, tiled=True)
    return jnp.sum(tiles, axis=0)


def one_axis_at_a_time(value, axes):
    return functools.reduce(lax.psum, axes, value)


def body(kernel, labels, start_dual, penalty, box):
    rows = kernel.shape[0]
    row_count = lax.axis_size(ROW)
    col_count = lax.axis_size(COL)
    ratio = row_count // col_count
    col_index = lax.axis_index(COL)
    piece = rows // col_count
    total = rows * row_count
    settings = box.shape[0]
    signs = labels.astype(jnp.float32)[:, None]
    first = jnp.minimum(jnp.maximum(start_dual, 0.0), box[None, :])
    signs = lax.dynamic_slice_in_dim(signs, col_index * piece, piece, 0)
    first = lax.dynamic_slice_in_dim(first, col_index * piece, piece, 0)

    def column_block(products):
        blocks = []
        for member in range(ratio):
            blocks.append(broadcast(products, ROW, ratio * col_index + member))
        return jnp.concatenate(blocks, axis=0)

    def iterate(step, carry):
        dual, scaled_mult, gap_rows, offset = carry
        weighted = (signs * dual).astype(jnp.bfloat16)
        gathered = collect(weighted, COL, 0)
        column = column_block(gathered)
        summed = sent_and_summed(
            jnp.dot(kernel, column, preferred_element_type=jnp.float32), COL, 0
        )
        q_value = signs * summed
        w_value = dual - scaled_mult - (q_value - 1.0) / penalty[None, :]
        local_bias = jnp.sum(signs * w_value, axis=0)
        offset = one_axis_at_a_time(local_bias, ROW_COL) / total
        hinge = jnp.maximum(0.0, 1.0 - q_value - signs * offset[None, :])
        gap_terms = dual * q_value - dual + box[None, :] * hinge
        local_gap = jnp.sum(gap_terms, axis=0)
        gap_rows = gap_rows.at[step].set(local_gap)
        x_value = w_value - signs * offset[None, :]
        dual_next = jnp.minimum(jnp.maximum(x_value + scaled_mult, 0.0), box[None, :])
        scaled_mult = scaled_mult + x_value - dual_next
        return (dual_next, scaled_mult, gap_rows, offset)

    start = (
        first,
        jnp.zeros_like(first),
        jnp.zeros((ITERS, settings), jnp.float32),
        jnp.zeros((settings,), jnp.float32),
    )
    dual, scaled_mult, gap_rows, offset = lax.fori_loop(0, ITERS, iterate, start)
    gap_rows = one_axis_at_a_time(gap_rows, ROW_COL) / total
    return (dual, scaled_mult, gap_rows, offset)


def solution(mesh):
    torus = Mesh(mesh.devices.reshape(4, 4, 2, 8, 2), ("row_0", "row_1", "row_2", "col_0", "col_1"))
    in_specs = (P(ROW, COL), P(ROW), P(ROW, None), P(), P())
    out_specs = (P(ROW_COL, None), P(ROW_COL, None), P(), P())
    return jax.shard_map(body, mesh=torus, in_specs=in_specs, out_specs=out_specs, check_vma=False)
```

profile of v0, /device:TPU:1, one launch (start us, length us, event | category | flops | bytes accessed | tf_op | source)
XLA Modules:
  0.0 503.2 jit_solution(10417138842678984312)
XLA Ops:
  8.7 447.4 %while.23 = (s32[]{:T(128)}, f32[40,128]{1,0:T(8,128)S(1)}, f32[40,128]{1,0:T(8,128)S(1)}, f32[3,128]{1,0:T(4,128)S(1)}, f32[128]{0:T(128)}, /*index=5*/f32[40,1...) while((s32[]{:T(128)}, f32[40,128]{1,0:T(8,128)S(1)}, ...), condition=%wide.region_10.11_spmd.clone, body=%wide.region_0.10_spmd.clone.sunk | while | flops 210581136 | bytes 21911424 | solution.py:99
  8.8 18.2 %all_to_all.28 = bf16[16,40,128]{2,1,0:T(8,128)(2,1)} all-to-all(bf16[16,40,128]{2,1,0:T(8,128)(2,1)S(1)} %broadcast_in_dim.45), channel_id=1, replica_groups=mesh['row_0'=4,'row_1'=4,'row_2'=2,'col_0'=8,'col_1'=2] {'col_0','col_1'}, dimensions={0} | all-to-all | bytes 327680 | tf_op jit(solution)/shard_map/while/body/eval_jaxpr/all_to_all | solution.py:21
  27.1 71.5 %all-gather.2.cloned.1.call-done = bf16[32,640,128]{2,1,0:T(8,128)(2,1)} async-done(((bf16[1,640,128]{2,1,0:T(8,128)(2,1)}), bf16[32,640,128]{2,1,0:T(8,128)(2,1)}) %all-gather.2.cloned.1.call-update) | async-done | bytes 5242896 | tf_op jit(solution)/shard_map/while/body/eval_jaxpr/all_gather | solution.py:16
  102.6 6.6 %all-to-all-start.1 = ((f32[16,40,128]{2,1,0:T(8,128)}), f32[16,40,128]{2,1,0:T(8,128)S(1)}, u32[]{:S(2)}, u32[]{:S(2)}) async-start(f32[16,40,128]{2,1,0:T(8,128)} %bitcast.29), calls=%async_computation.1 | async-start | bytes 655360 | tf_op jit(solution)/shard_map/while/body/eval_jaxpr/all_to_all | solution.py:44
  110.0 11.7 %all-to-all-done.1 = f32[16,40,128]{2,1,0:T(8,128)S(1)} async-done(((f32[16,40,128]{2,1,0:T(8,128)}), f32[16,40,128]{2,1,0:T(8,128)S(1)}, u32[]{:S(2)}, u32[]{:S(2)}) %all-to-all-start.1) | async-done | bytes 327712 | tf_op jit(solution)/shard_map/while/body/eval_jaxpr/all_to_all | solution.py:44
  121.7 9.3 %psum.120 = f32[128]{0:T(128)S(1)} all-reduce(f32[128]{0:T(128)S(1)} %get-tuple-element.420), channel_id=1, replica_groups=mesh['row_0'=4,'row_1'=4,'row_2'=2,'col_0'=8,'col_1'=2] {'row_0'}, use_global_device_ids=true, to_apply=%region_3.3 | all-reduce | flops 128 | bytes 1024 | tf_op jit(solution)/shard_map/while/body/eval_jaxpr/psum | solution.py:49
  131.0 8.4 %psum.121 = f32[128]{0:T(128)S(1)} all-reduce(f32[128]{0:T(128)S(1)} %psum.120), channel_id=1, replica_groups=mesh['row_0'=4,'row_1'=4,'row_2'=2,'col_0'=8,'col_1'=2] {'row_1'}, use_global_device_ids=true, to_apply=%region_4.4 | all-reduce | flops 128 | bytes 1024 | tf_op jit(solution)/shard_map/while/body/eval_jaxpr/psum | solution.py:49
  139.4 7.8 %psum.122 = f32[128]{0:T(128)S(1)} all-reduce(f32[128]{0:T(128)S(1)} %psum.121), channel_id=1, replica_groups=mesh['row_0'=4,'row_1'=4,'row_2'=2,'col_0'=8,'col_1'=2] {'row_2'}, use_global_device_ids=true, to_apply=%region_5.5 | all-reduce | flops 128 | bytes 1024 | tf_op jit(solution)/shard_map/while/body/eval_jaxpr/psum | solution.py:49
  147.3 10.8 %psum.123 = f32[128]{0:T(128)S(1)} all-reduce(f32[128]{0:T(128)S(1)} %psum.122), channel_id=1, replica_groups=mesh['row_0'=4,'row_1'=4,'row_2'=2,'col_0'=8,'col_1'=2] {'col_0'}, use_global_device_ids=true, to_apply=%region_6.6 | all-reduce | flops 128 | bytes 1024 | tf_op jit(solution)/shard_map/while/body/eval_jaxpr/psum | solution.py:49
  158.0 3.8 psum.124
  162.7 13.6 %all_to_all.28 = bf16[16,40,128]{2,1,0:T(8,128)(2,1)} all-to-all(bf16[16,40,128]{2,1,0:T(8,128)(2,1)S(1)} %broadcast_in_dim.45), channel_id=1, replica_groups=mesh['row_0'=4,'row_1'=4,'row_2'=2,'col_0'=8,'col_1'=2] {'col_0','col_1'}, dimensions={0} | all-to-all | bytes 327680 | tf_op jit(solution)/shard_map/while/body/eval_jaxpr/all_to_all | solution.py:21
  176.3 69.1 %all-gather.2.cloned.1.call-done = bf16[32,640,128]{2,1,0:T(8,128)(2,1)} async-done(((bf16[1,640,128]{2,1,0:T(8,128)(2,1)}), bf16[32,640,128]{2,1,0:T(8,128)(2,1)}) %all-gather.2.cloned.1.call-update) | async-done | bytes 5242896 | tf_op jit(solution)/shard_map/while/body/eval_jaxpr/all_gather | solution.py:16
  249.4 6.6 %all-to-all-start.1 = ((f32[16,40,128]{2,1,0:T(8,128)}), f32[16,40,128]{2,1,0:T(8,128)S(1)}, u32[]{:S(2)}, u32[]{:S(2)}) async-start(f32[16,40,128]{2,1,0:T(8,128)} %bitcast.29), calls=%async_computation.1 | async-start | bytes 655360 | tf_op jit(solution)/shard_map/while/body/eval_jaxpr/all_to_all | solution.py:44
  256.7 11.7 %all-to-all-done.1 = f32[16,40,128]{2,1,0:T(8,128)S(1)} async-done(((f32[16,40,128]{2,1,0:T(8,128)}), f32[16,40,128]{2,1,0:T(8,128)S(1)}, u32[]{:S(2)}, u32[]{:S(2)}) %all-to-all-start.1) | async-done | bytes 327712 | tf_op jit(solution)/shard_map/while/body/eval_jaxpr/all_to_all | solution.py:44
  268.5 9.3 %psum.120 = f32[128]{0:T(128)S(1)} all-reduce(f32[128]{0:T(128)S(1)} %get-tuple-element.420), channel_id=1, replica_groups=mesh['row_0'=4,'row_1'=4,'row_2'=2,'col_0'=8,'col_1'=2] {'row_0'}, use_global_device_ids=true, to_apply=%region_3.3 | all-reduce | flops 128 | bytes 1024 | tf_op jit(solution)/shard_map/while/body/eval_jaxpr/psum | solution.py:49
  277.8 8.4 %psum.121 = f32[128]{0:T(128)S(1)} all-reduce(f32[128]{0:T(128)S(1)} %psum.120), channel_id=1, replica_groups=mesh['row_0'=4,'row_1'=4,'row_2'=2,'col_0'=8,'col_1'=2] {'row_1'}, use_global_device_ids=true, to_apply=%region_4.4 | all-reduce | flops 128 | bytes 1024 | tf_op jit(solution)/shard_map/while/body/eval_jaxpr/psum | solution.py:49
  286.2 7.8 %psum.122 = f32[128]{0:T(128)S(1)} all-reduce(f32[128]{0:T(128)S(1)} %psum.121), channel_id=1, replica_groups=mesh['row_0'=4,'row_1'=4,'row_2'=2,'col_0'=8,'col_1'=2] {'row_2'}, use_global_device_ids=true, to_apply=%region_5.5 | all-reduce | flops 128 | bytes 1024 | tf_op jit(solution)/shard_map/while/body/eval_jaxpr/psum | solution.py:49
  294.0 10.8 %psum.123 = f32[128]{0:T(128)S(1)} all-reduce(f32[128]{0:T(128)S(1)} %psum.122), channel_id=1, replica_groups=mesh['row_0'=4,'row_1'=4,'row_2'=2,'col_0'=8,'col_1'=2] {'col_0'}, use_global_device_ids=true, to_apply=%region_6.6 | all-reduce | flops 128 | bytes 1024 | tf_op jit(solution)/shard_map/while/body/eval_jaxpr/psum | solution.py:49
  304.8 3.8 psum.124
  309.5 13.6 %all_to_all.28 = bf16[16,40,128]{2,1,0:T(8,128)(2,1)} all-to-all(bf16[16,40,128]{2,1,0:T(8,128)(2,1)S(1)} %broadcast_in_dim.45), channel_id=1, replica_groups=mesh['row_0'=4,'row_1'=4,'row_2'=2,'col_0'=8,'col_1'=2] {'col_0','col_1'}, dimensions={0} | all-to-all | bytes 327680 | tf_op jit(solution)/shard_map/while/body/eval_jaxpr/all_to_all | solution.py:21
  323.1 69.1 %all-gather.2.cloned.1.call-done = bf16[32,640,128]{2,1,0:T(8,128)(2,1)} async-done(((bf16[1,640,128]{2,1,0:T(8,128)(2,1)}), bf16[32,640,128]{2,1,0:T(8,128)(2,1)}) %all-gather.2.cloned.1.call-update) | async-done | bytes 5242896 | tf_op jit(solution)/shard_map/while/body/eval_jaxpr/all_gather | solution.py:16
  396.2 6.6 %all-to-all-start.1 = ((f32[16,40,128]{2,1,0:T(8,128)}), f32[16,40,128]{2,1,0:T(8,128)S(1)}, u32[]{:S(2)}, u32[]{:S(2)}) async-start(f32[16,40,128]{2,1,0:T(8,128)} %bitcast.29), calls=%async_computation.1 | async-start | bytes 655360 | tf_op jit(solution)/shard_map/while/body/eval_jaxpr/all_to_all | solution.py:44
  403.5 11.7 %all-to-all-done.1 = f32[16,40,128]{2,1,0:T(8,128)S(1)} async-done(((f32[16,40,128]{2,1,0:T(8,128)}), f32[16,40,128]{2,1,0:T(8,128)S(1)}, u32[]{:S(2)}, u32[]{:S(2)}) %all-to-all-start.1) | async-done | bytes 327712 | tf_op jit(solution)/shard_map/while/body/eval_jaxpr/all_to_all | solution.py:44
  415.3 9.3 %psum.120 = f32[128]{0:T(128)S(1)} all-reduce(f32[128]{0:T(128)S(1)} %get-tuple-element.420), channel_id=1, replica_groups=mesh['row_0'=4,'row_1'=4,'row_2'=2,'col_0'=8,'col_1'=2] {'row_0'}, use_global_device_ids=true, to_apply=%region_3.3 | all-reduce | flops 128 | bytes 1024 | tf_op jit(solution)/shard_map/while/body/eval_jaxpr/psum | solution.py:49
  424.6 8.4 %psum.121 = f32[128]{0:T(128)S(1)} all-reduce(f32[128]{0:T(128)S(1)} %psum.120), channel_id=1, replica_groups=mesh['row_0'=4,'row_1'=4,'row_2'=2,'col_0'=8,'col_1'=2] {'row_1'}, use_global_device_ids=true, to_apply=%region_4.4 | all-reduce | flops 128 | bytes 1024 | tf_op jit(solution)/shard_map/while/body/eval_jaxpr/psum | solution.py:49
  433.0 7.8 %psum.122 = f32[128]{0:T(128)S(1)} all-reduce(f32[128]{0:T(128)S(1)} %psum.121), channel_id=1, replica_groups=mesh['row_0'=4,'row_1'=4,'row_2'=2,'col_0'=8,'col_1'=2] {'row_2'}, use_global_device_ids=true, to_apply=%region_5.5 | all-reduce | flops 128 | bytes 1024 | tf_op jit(solution)/shard_map/while/body/eval_jaxpr/psum | solution.py:49
  440.8 10.8 %psum.123 = f32[128]{0:T(128)S(1)} all-reduce(f32[128]{0:T(128)S(1)} %psum.122), channel_id=1, replica_groups=mesh['row_0'=4,'row_1'=4,'row_2'=2,'col_0'=8,'col_1'=2] {'col_0'}, use_global_device_ids=true, to_apply=%region_6.6 | all-reduce | flops 128 | bytes 1024 | tf_op jit(solution)/shard_map/while/body/eval_jaxpr/psum | solution.py:49
  451.6 3.8 psum.124
  456.1 7.1 %psum.105 = f32[3,128]{1,0:T(4,128)S(1)} all-reduce(f32[3,128]{1,0:T(4,128)S(1)} %get-tuple-element.279), channel_id=1, replica_groups=mesh['row_0'=4,'row_1'=4,'row_2'=2,'col_0'=8,'col_1'=2] {'row_0'}, use_global_device_ids=true, to_apply=%region_11.12 | all-reduce | flops 384 | bytes 3072 | tf_op jit(solution)/shard_map/psum | solution.py:49
  463.2 6.0 %psum.106 = f32[3,128]{1,0:T(4,128)S(1)} all-reduce(f32[3,128]{1,0:T(4,128)S(1)} %psum.105), channel_id=1, replica_groups=mesh['row_0'=4,'row_1'=4,'row_2'=2,'col_0'=8,'col_1'=2] {'row_1'}, use_global_device_ids=true, to_apply=%region_12.13 | all-reduce | flops 384 | bytes 3072 | tf_op jit(solution)/shard_map/psum | solution.py:49
  469.2 11.1 %psum.107 = f32[3,128]{1,0:T(4,128)S(1)} all-reduce(f32[3,128]{1,0:T(4,128)S(1)} %psum.106), channel_id=1, replica_groups=mesh['row_0'=4,'row_1'=4,'row_2'=2,'col_0'=8,'col_1'=2] {'row_2'}, use_global_device_ids=true, to_apply=%region_13.14 | all-reduce | flops 384 | bytes 3072 | tf_op jit(solution)/shard_map/psum | solution.py:49
  480.3 12.0 %psum.108 = f32[3,128]{1,0:T(4,128)S(1)} all-reduce(f32[3,128]{1,0:T(4,128)S(1)} %psum.107), channel_id=1, replica_groups=mesh['row_0'=4,'row_1'=4,'row_2'=2,'col_0'=8,'col_1'=2] {'col_0'}, use_global_device_ids=true, to_apply=%region_14.15 | all-reduce | flops 384 | bytes 3072 | tf_op jit(solution)/shard_map/psum | solution.py:49
  (78 shorter events, 23.0 us)
Async XLA Ops:
  8.7 89.9 %all-gather.2.cloned.1.call-start = ((), (), s32[]{:S(2)}) async-start(), calls=%async_computation.2 | async-start | bytes 5406720 | tf_op jit(solution)/shard_map/while/body/eval_jaxpr/all_gather | solution.py:16
  99.6 9.6 %copy-start.5 = (s32[2]{0:T(128)S(1)}, s32[2]{0:T(128)}, u32[]{:S(2)}) copy-start(s32[2]{0:T(128)} %get-tuple-element.470) | copy-start | bytes 28 | tf_op jit(solution)/shard_map/while
  99.6 22.0 %copy-start.3 = (f32[128]{0:T(128)S(1)}, f32[128]{0:T(128)}, u32[]{:S(2)}) copy-start(f32[128]{0:T(128)} %get-tuple-element.465) | copy-start | bytes 1540 | tf_op jit(solution)/shard_map/while
  99.6 62.1 %copy-start.2 = (f32[128]{0:T(128)S(1)}, f32[128]{0:T(128)}, u32[]{:S(2)}) copy-start(f32[128]{0:T(128)} %get-tuple-element.466) | copy-start | bytes 1540 | tf_op jit(solution)/shard_map/while
  102.6 19.0 %all-to-all-start.1 = ((f32[16,40,128]{2,1,0:T(8,128)}), f32[16,40,128]{2,1,0:T(8,128)S(1)}, u32[]{:S(2)}, u32[]{:S(2)}) async-start(f32[16,40,128]{2,1,0:T(8,128)} %bitcast.29), calls=%async_computation.1 | async-start | bytes 655360 | tf_op jit(solution)/shard_map/while/body/eval_jaxpr/all_to_all | solution.py:44
  161.8 0.7 copy-start.4
  162.5 82.9 %all-gather.2.cloned.1.call-start = ((), (), s32[]{:S(2)}) async-start(), calls=%async_computation.2 | async-start | bytes 5406720 | tf_op jit(solution)/shard_map/while/body/eval_jaxpr/all_gather | solution.py:16
  246.4 9.6 %copy-start.5 = (s32[2]{0:T(128)S(1)}, s32[2]{0:T(128)}, u32[]{:S(2)}) copy-start(s32[2]{0:T(128)} %get-tuple-element.470) | copy-start | bytes 28 | tf_op jit(solution)/shard_map/while
  246.4 22.0 %copy-start.3 = (f32[128]{0:T(128)S(1)}, f32[128]{0:T(128)}, u32[]{:S(2)}) copy-start(f32[128]{0:T(128)} %get-tuple-element.465) | copy-start | bytes 1540 | tf_op jit(solution)/shard_map/while
  246.4 62.1 %copy-start.2 = (f32[128]{0:T(128)S(1)}, f32[128]{0:T(128)}, u32[]{:S(2)}) copy-start(f32[128]{0:T(128)} %get-tuple-element.466) | copy-start | bytes 1540 | tf_op jit(solution)/shard_map/while
  249.4 19.0 %all-to-all-start.1 = ((f32[16,40,128]{2,1,0:T(8,128)}), f32[16,40,128]{2,1,0:T(8,128)S(1)}, u32[]{:S(2)}, u32[]{:S(2)}) async-start(f32[16,40,128]{2,1,0:T(8,128)} %bitcast.29), calls=%async_computation.1 | async-start | bytes 655360 | tf_op jit(solution)/shard_map/while/body/eval_jaxpr/all_to_all | solution.py:44
  308.6 0.7 copy-start.4
  309.3 82.9 %all-gather.2.cloned.1.call-start = ((), (), s32[]{:S(2)}) async-start(), calls=%async_computation.2 | async-start | bytes 5406720 | tf_op jit(solution)/shard_map/while/body/eval_jaxpr/all_gather | solution.py:16
  393.2 9.6 %copy-start.5 = (s32[2]{0:T(128)S(1)}, s32[2]{0:T(128)}, u32[]{:S(2)}) copy-start(s32[2]{0:T(128)} %get-tuple-element.470) | copy-start | bytes 28 | tf_op jit(solution)/shard_map/while
  393.2 22.0 %copy-start.3 = (f32[128]{0:T(128)S(1)}, f32[128]{0:T(128)}, u32[]{:S(2)}) copy-start(f32[128]{0:T(128)} %get-tuple-element.465) | copy-start | bytes 1540 | tf_op jit(solution)/shard_map/while
  393.2 62.1 %copy-start.2 = (f32[128]{0:T(128)S(1)}, f32[128]{0:T(128)}, u32[]{:S(2)}) copy-start(f32[128]{0:T(128)} %get-tuple-element.466) | copy-start | bytes 1540 | tf_op jit(solution)/shard_map/while
  396.2 19.0 %all-to-all-start.1 = ((f32[16,40,128]{2,1,0:T(8,128)}), f32[16,40,128]{2,1,0:T(8,128)S(1)}, u32[]{:S(2)}, u32[]{:S(2)}) async-start(f32[16,40,128]{2,1,0:T(8,128)} %bitcast.29), calls=%async_computation.1 | async-start | bytes 655360 | tf_op jit(solution)/shard_map/while/body/eval_jaxpr/all_to_all | solution.py:44
  455.4 0.7 copy-start.4
  456.1 40.6 %copy-start = (f32[40,128]{1,0:T(8,128)}, f32[40,128]{1,0:T(8,128)S(1)}, u32[]{:S(2)}) copy-start(f32[40,128]{1,0:T(8,128)S(1)} %get-tuple-element.273) | copy-start | bytes 61444
  456.1 40.6 %copy-start.1 = (f32[40,128]{1,0:T(8,128)}, f32[40,128]{1,0:T(8,128)S(1)}, u32[]{:S(2)}) copy-start(f32[40,128]{1,0:T(8,128)S(1)} %get-tuple-element.274) | copy-start | bytes 61444
Sparse Core Ops, SparseCore 0:
  27.2 71.3 all-gather.1
  176.4 68.8 all-gather.1
  323.2 68.8 all-gather.1
where the time goes:
time: 509 us; the launch traced here: 503 us
  waiting for transfers between devices  245 us (48%)
  blocking collectives  205 us (40%)
  starting transfers between devices  19.9 us (4%)
  between operations  13.7 us (3%)
  other arithmetic  6.74 us (1%)
  matrix products  6.3 us (1%)
  local copies, waits for them, and re-layouts  6.04 us (1%)
    all_gather x3, waiting for transfers between devices, broadcast(): lax.all_gather(value, axis)  210 us
    psum x20, blocking collectives, one_axis_at_a_time(): return functools.reduce(lax.psum, axes, value)  160 us
    all_to_all x3, blocking collectives, from_everyone(): lax.all_to_all(jnp.broadcast_to(value[None], (length, *value.shape)), axi...  45.5 us
    all_to_all x3, waiting for transfers between devices, sent_and_summed(): lax.all_to_all(cut_along(value, dim, length), axis, 0, 0, tiled=True)  35 us
    all_to_all x3, starting transfers between devices, sent_and_summed(): lax.all_to_all(cut_along(value, dim, length), axis, 0, 0, tiled=True)  19.8 us
  transfers between devices with their start and end apart: 6, of which 6 were waited for; matrix products, arithmetic and copies ran while one was open for 0% of the time, Pallas kernels for 0%

commit v1 on v0

v1 whole, which is shorter than its diff:
```python
import functools

import jax
import jax.numpy as jnp
from jax import lax
from jax.experimental import pallas as pl
from jax.experimental.pallas import tpu as pltpu
from jax.sharding import Mesh
from jax.sharding import PartitionSpec as P

ITERS = 3
ROW = ("row_0", "row_1", "row_2")
COL = ("col_0", "col_1")
ROW_COL = ROW + COL
MESH = pl.DeviceIdType.MESH
F32 = jnp.float32
BF16 = jnp.bfloat16


def loop(low, high, step):
    def one(i, carry):
        step(i)
        return carry

    lax.fori_loop(low, high, one, jnp.int32(0))


def remote(src, dst, send, recv, device):
    return pltpu.make_async_remote_copy(
        src_ref=src, dst_ref=dst, send_sem=send, recv_sem=recv, device_id=device, device_id_type=MESH
    )


def admm(
    dims, total,
    kernel_hbm, labels_hbm, start_hbm, penalty_ref, box_ref,
    dual_out, mult_out, gaps_out, offset_out,
    kernel_ref, labels_ref, start_ref, signs_ref, part_ref, load_sem,
    state_send, state_recv, state_ss, state_rs,
    core_send, core_recv, core_ss, core_rs,
    row_send, row_recv, row_ss, row_rs,
    gat_ref, gat_ss, gat_rs, fwd_ss,
    col_send, col_recv, col_ss, col_rs,
    pcol_ref, pcol_ss, pcol_rs,
    near_ref, near_ss, near_rs,
    far_ref, far_ss, far_rs,
):
    hs, xs, ks, ys, ls = dims
    groups, rows, cols = hs * xs, hs * xs * ks, ys * ls
    h, x, k = (lax.axis_index(a) for a in ROW)
    y, l = (lax.axis_index(a) for a in COL)
    g = h * xs + x
    r = g * ks + k
    c = y * ls + l
    piece = state_send.shape[2]
    near_n, far_n = ys * ks, hs * xs * ls
    near_me = y * ks + k
    far_me = g * ls + l
    other = 1 - k

    def chip(to):
        return {"row_0": lax.div(to, xs), "row_1": lax.rem(to, xs)}

    def column(to):
        return {"col_0": lax.div(to, ls), "col_1": lax.rem(to, ls)}

    def whole(row, col):
        return {
            "row_0": lax.div(row, xs * ks), "row_1": lax.rem(lax.div(row, ks), xs), "row_2": lax.rem(row, ks),
            "col_0": lax.div(col, ls), "col_1": lax.rem(col, ls),
        }

    def near(to):
        return {"col_0": lax.div(to, ks), "row_2": lax.rem(to, ks)}

    def far(to):
        return {
            "row_0": lax.div(to, xs * ls), "row_1": lax.rem(lax.div(to, ls), xs), "col_1": lax.rem(to, ls)
        }

    partner = {"row_2": other}
    mine = g * ks + other
    block = r * cols + c
    to_piece = lax.rem(block, rows)
    to_column = whole(
        lax.div(to_piece, ks) * ks + (ks - 1 - lax.rem(to_piece, ks)), lax.div(block, rows)
    )
    owned = c * rows + mine
    to_row = whole(lax.div(owned, cols), lax.rem(owned, cols))

    load_k = pltpu.make_async_copy(kernel_hbm, kernel_ref, load_sem.at[0])
    load_s = pltpu.make_async_copy(start_hbm, start_ref, load_sem.at[1])
    load_l = pltpu.make_async_copy(labels_hbm, labels_ref, load_sem.at[2])
    load_l.start()
    load_s.start()
    load_k.start()

    barrier = pltpu.get_barrier_semaphore()

    def greet(device):
        pl.semaphore_signal(barrier, inc=1, device_id=device, device_id_type=MESH)

    greet(to_column)
    greet(to_row)
    loop(1, far_n, lambda i: greet(far(lax.rem(far_me + i, far_n))))
    loop(1, near_n, lambda i: greet(near(lax.rem(near_me + i, near_n))))
    crossed = ys * (ls - 1)
    if crossed:
        def cross(i):
            greet({"col_0": lax.rem(i, ys), "col_1": lax.rem(l + 1 + lax.div(i, ys), ls)})
        loop(0, crossed, cross)

    penalty = penalty_ref[...]
    box = box_ref[...]
    load_l.wait()
    load_s.wait()
    wide = labels_ref.shape[1]
    for i in range(labels_ref.shape[0]):
        line = labels_ref[i : i + 1, :].astype(F32)
        if wide == 128:
            block_signs = jnp.transpose(jnp.broadcast_to(line, (128, 128)))
        else:
            block_signs = jnp.broadcast_to(jnp.transpose(line), (wide, 128))
        signs_ref[i * wide : (i + 1) * wide, :] = block_signs
    first = jnp.minimum(jnp.maximum(start_ref[...], 0.0), box)
    start_ref[...] = first
    weighted = (signs_ref[...] * first).astype(BF16)
    own_rows = pl.ds(pl.multiple_of(c * piece, 8), piece)
    signs_row = signs_ref[own_rows, :]
    dual = start_ref[own_rows, :]
    mult = jnp.zeros_like(dual)
    state_send[0, 0] = dual
    state_send[0, 1] = signs_row

    def move_state(t, device):
        remote(state_send.at[t], state_recv.at[t], state_ss.at[t], state_rs.at[t], device).start()

    def arrived_state(t):
        remote(state_send.at[t], state_recv.at[t], state_ss.at[t], state_rs.at[t], to_row).wait_recv()
        return state_recv[t, 0], state_recv[t, 1]

    def near_copy(t, i):
        return remote(near_ref.at[t, near_me], near_ref.at[t, near_me], near_ss.at[t, i], near_rs.at[t, near_me], near(i))

    def near_wait(t, i):
        return remote(near_ref.at[t, i], near_ref.at[t, i], near_ss.at[t, i], near_rs.at[t, i], near(i))

    def far_copy(t, i):
        return remote(far_ref.at[t, far_me], far_ref.at[t, far_me], far_ss.at[t, i], far_rs.at[t, far_me], far(i))

    def far_wait(t, i):
        return remote(far_ref.at[t, i], far_ref.at[t, i], far_ss.at[t, i], far_rs.at[t, i], far(i))

    def sum_start(t, top, bottom):
        near_ref[t, near_me, 0:1, :] = top
        near_ref[t, near_me, 1:2, :] = bottom
        loop(1, near_n, lambda i: near_copy(t, lax.rem(near_me + i, near_n)).start())

    def sum_middle(t):
        loop(1, near_n, lambda i: near_wait(t, lax.rem(near_me + i, near_n)).wait_recv())
        far_ref[t, far_me] = jnp.sum(near_ref[t], axis=0)
        loop(1, far_n, lambda i: far_copy(t, lax.rem(far_me + i, far_n)).start())

    def sum_end(t):
        loop(1, far_n, lambda i: far_wait(t, lax.rem(far_me + i, far_n)).wait_recv())
        return jnp.sum(far_ref[t], axis=0)

    def local_bias(dual, mult, signs, product_sum):
        steady = jnp.sum(signs * (dual - mult), axis=0, keepdims=True)
        return steady - (product_sum - jnp.sum(signs, axis=0, keepdims=True)) / penalty

    def update(q, dual, mult, signs, offset):
        w = dual - mult - (q - 1.0) / penalty
        hinge = jnp.maximum(0.0, 1.0 - q - signs * offset)
        gap = jnp.sum(dual * q - dual + box * hinge, axis=0, keepdims=True)
        x_value = w - signs * offset
        dual_next = jnp.minimum(jnp.maximum(x_value + mult, 0.0), box)
        return dual_next, mult + x_value - dual_next, gap

    def row_copy(s, i):
        return remote(row_send.at[s, i], row_recv.at[s, g], row_ss.at[s, i], row_rs.at[s, g], chip(i))

    def row_wait(s, i):
        return remote(row_send.at[s, i], row_recv.at[s, i], row_ss.at[s, i], row_rs.at[s, i], chip(i))

    def core_copy(s):
        return remote(core_send.at[s], core_recv.at[s], core_ss.at[s], core_rs.at[s], partner)

    def transposed_start(s, weighted):
        product = lax.dot_general(
            kernel_ref[...], weighted, (((0,), (0,)), ((), ())), preferred_element_type=F32
        )
        part_ref[...] = product.reshape(part_ref.shape)
        core_send[s] = part_ref[:, k].astype(BF16)
        return jnp.sum(product, axis=0, keepdims=True)

    def transposed_send(s):
        core_copy(s).wait_recv()
        both = part_ref[:, other] + core_recv[s].astype(F32)
        part_ref[:, other] = both
        row_send[s] = both.astype(BF16)
        loop(1, groups, lambda i: row_copy(s, lax.rem(g + i, groups)).start())

    def transposed_sum(s):
        row_recv[s, g] = jnp.zeros(row_recv.shape[2:], BF16)
        loop(1, groups, lambda i: row_wait(s, lax.rem(g + i, groups)).wait_recv())
        return part_ref[g, other] + jnp.sum(row_recv[s].astype(F32), axis=0)

    zero = jnp.zeros((1, box.shape[1]), F32)

    load_k.wait()
    product_sum = transposed_start(0, weighted)
    pl.semaphore_wait(barrier, 2 + far_n - 1 + near_n - 1 + crossed)
    core_copy(0).start()
    sum_start(0, local_bias(dual, mult, signs_row, product_sum), zero)
    move_state(0, to_column)
    transposed_send(0)
    sum_middle(0)
    q_sum = transposed_sum(0)
    dual, signs_col = arrived_state(0)
    mult = jnp.zeros_like(dual)
    offset = sum_end(0)[0:1] / total
    dual, mult, gap = update(signs_col * q_sum, dual, mult, signs_col, offset)

    gat_ref[mine] = (signs_col * dual).astype(BF16)

    def gat_copy(slot, send, device):
        return remote(gat_ref.at[slot], gat_ref.at[slot], send, gat_rs.at[slot], device)

    loop(1, groups, lambda i: gat_copy(mine, gat_ss.at[lax.rem(g + i, groups)], chip(lax.rem(g + i, groups))).start())
    gat_copy(mine, fwd_ss.at[g], partner).start()
    state_send[1, 0] = dual
    state_send[1, 1] = mult
    move_state(1, to_row)

    def forward(i):
        to = lax.rem(g + i, groups)
        slot = to * ks + other
        gat_copy(slot, fwd_ss.at[to], partner).wait_recv()
        gat_copy(slot, fwd_ss.at[to], partner).start()

    loop(1, groups, forward)
    loop(0, groups, lambda i: gat_copy(i * ks + k, fwd_ss.at[i], partner).wait_recv())
    gathered = gat_ref[...].astype(F32).reshape(rows * piece, -1).astype(BF16)
    product = jnp.dot(kernel_ref[...], gathered, preferred_element_type=F32)
    col_send[...] = product.reshape(col_send.shape).astype(BF16)
    part_ref[0 : cols // ks] = product.reshape(cols // ks, ks, piece, -1)

    def col_copy(i):
        return remote(col_send.at[i], col_recv.at[c], col_ss.at[i], col_rs.at[c], column(i))

    def col_wait(i):
        return remote(col_send.at[i], col_recv.at[i], col_ss.at[i], col_rs.at[i], column(i))

    sum_start(1, local_bias(dual, mult, signs_col, jnp.sum(product, axis=0, keepdims=True)), gap)
    loop(1, cols, lambda i: col_copy(lax.rem(c + i, cols)).start())
    sum_middle(1)
    col_recv[c] = jnp.zeros(col_recv.shape[1:], BF16)
    loop(1, cols, lambda i: col_wait(lax.rem(c + i, cols)).wait_recv())
    q_sum = part_ref[lax.div(c, ks), lax.rem(c, ks)] + jnp.sum(col_recv[...].astype(F32), axis=0)
    dual, mult = arrived_state(1)
    sums = sum_end(1)
    gaps_out[0:1, :] = sums[1:2] / total
    offset = sums[0:1] / total
    dual, mult, gap = update(signs_row * q_sum, dual, mult, signs_row, offset)

    pcol_ref[c] = (signs_row * dual).astype(BF16)

    def pcol_copy(i):
        return remote(pcol_ref.at[c], pcol_ref.at[c], pcol_ss.at[i], pcol_rs.at[c], column(i))

    def pcol_wait(i):
        return remote(pcol_ref.at[i], pcol_ref.at[i], pcol_ss.at[i], pcol_rs.at[i], column(i))

    loop(1, cols, lambda i: pcol_copy(lax.rem(c + i, cols)).start())
    state_send[2, 0] = dual
    state_send[2, 1] = mult
    move_state(2, to_column)
    loop(1, cols, lambda i: pcol_wait(lax.rem(c + i, cols)).wait_recv())
    weighted = pcol_ref[...].astype(F32).reshape(cols * piece, -1).astype(BF16)
    product_sum = transposed_start(1, weighted)
    core_copy(1).start()
    sum_start(2, local_bias(dual, mult, signs_row, product_sum), gap)
    transposed_send(1)
    sum_middle(2)
    q_sum = transposed_sum(1)
    dual, mult = arrived_state(2)
    sums = sum_end(2)
    gaps_out[1:2, :] = sums[1:2] / total
    offset = sums[0:1] / total
    dual, mult, gap = update(signs_col * q_sum, dual, mult, signs_col, offset)

    sum_start(3, zero, gap)
    state_send[3, 0] = dual
    state_send[3, 1] = mult
    move_state(3, to_row)
    offset_out[...] = offset
    sum_middle(3)
    dual, mult = arrived_state(3)
    dual_out[...] = dual
    mult_out[...] = mult
    gaps_out[2:3, :] = sum_end(3)[1:2] / total

    for t in range(4):
        remote(state_send.at[t], state_recv.at[t], state_ss.at[t], state_rs.at[t], to_row).wait_send()
        loop(1, near_n, lambda i: near_wait(t, lax.rem(near_me + i, near_n)).wait_send())
        loop(1, far_n, lambda i: far_wait(t, lax.rem(far_me + i, far_n)).wait_send())
    for s in range(2):
        core_copy(s).wait_send()
        loop(1, groups, lambda i: row_wait(s, lax.rem(g + i, groups)).wait_send())
    loop(1, groups, lambda i: gat_copy(mine, gat_ss.at[lax.rem(g + i, groups)], partner).wait_send())
    loop(0, groups, lambda i: gat_copy(i * ks + other, fwd_ss.at[i], partner).wait_send())
    loop(1, cols, lambda i: col_wait(lax.rem(c + i, cols)).wait_send())
    loop(1, cols, lambda i: pcol_wait(lax.rem(c + i, cols)).wait_send())


def body(dims, kernel, labels, start_dual, penalty, box):
    hs, xs, ks, ys, ls = dims
    groups, rows, cols = hs * xs, hs * xs * ks, ys * ls
    height, width = kernel.shape
    settings = box.shape[0]
    piece = height // cols
    total = height * rows
    near_n, far_n = ys * ks, hs * xs * ls
    wide = 128 if height % 128 == 0 else height
    dma = pltpu.SemaphoreType.DMA
    vmem = pltpu.VMEM
    scratch = [
        vmem((height, width), BF16), vmem((height // wide, wide), jnp.int32), vmem((height, settings), F32),
        vmem((height, settings), F32), vmem((groups, ks, piece, settings), F32), dma((3,)),
        vmem((4, 2, piece, settings), F32), vmem((4, 2, piece, settings), F32), dma((4,)), dma((4,)),
        vmem((2, groups, piece, settings), BF16), vmem((2, groups, piece, settings), BF16), dma((2,)), dma((2,)),
        vmem((2, groups, piece, settings), BF16), vmem((2, groups, piece, settings), BF16), dma((2, groups)), dma((2, groups)),
        vmem((rows, piece, settings), BF16), dma((groups,)), dma((rows,)), dma((groups,)),
        vmem((cols, piece, settings), BF16), vmem((cols, piece, settings), BF16), dma((cols,)), dma((cols,)),
        vmem((cols, piece, settings), BF16), dma((cols,)), dma((cols,)),
        vmem((4, near_n, 2, settings), F32), dma((4, near_n)), dma((4, near_n)),
        vmem((4, far_n, 2, settings), F32), dma((4, far_n)), dma((4, far_n)),
    ]
    in_vmem = pl.BlockSpec(memory_space=vmem)
    in_hbm = pl.BlockSpec(memory_space=pltpu.HBM)
    dual, mult, gaps, offset = pl.pallas_call(
        functools.partial(admm, dims, total),
        out_shape=(
            jax.ShapeDtypeStruct((piece, settings), F32), jax.ShapeDtypeStruct((piece, settings), F32),
            jax.ShapeDtypeStruct((ITERS, settings), F32), jax.ShapeDtypeStruct((1, settings), F32),
        ),
        in_specs=[in_hbm, in_hbm, in_hbm, in_vmem, in_vmem],
        out_specs=(in_vmem,) * 4,
        scratch_shapes=scratch,
        compiler_params=pltpu.CompilerParams(collective_id=0, has_side_effects=True),
        name="admm",
    )(kernel, labels.reshape(height // wide, wide), start_dual, penalty[None, :], box[None, :])
    return dual, mult, gaps, offset[0]


def build(torus):
    dims = torus.devices.shape
    in_specs = (P(ROW, COL), P(ROW), P(ROW, None), P(), P())
    out_specs = (P(ROW_COL, None), P(ROW_COL, None), P(), P())
    return jax.shard_map(
        functools.partial(body, dims), mesh=torus, in_specs=in_specs, out_specs=out_specs, check_vma=False
    )


def solution(mesh):
    return build(Mesh(mesh.devices.reshape(4, 4, 2, 8, 2), ROW_COL))
```

time: 509 us -> 102 us (0.20); the launches traced: 503 us -> 102 us
  waiting for transfers between devices: 245 us -> 0 us
  blocking collectives: 205 us -> 0 us
  Pallas kernels: 0 us -> 96.3 us
  starting transfers between devices: 19.9 us -> 0 us
  between operations: 13.7 us -> 0.64 us
  other arithmetic: 6.74 us -> 0 us
  matrix products: 6.3 us -> 0 us
    all_gather x3 -> x0, waiting for transfers between devices: 210 us -> none  [broadcast(): lax.all_gather(value, axis)]
    psum x20 -> x0, blocking collectives: 160 us -> none  [one_axis_at_a_time(): return functools.reduce(lax.psum, axes, value)]
    pallas_call x0 -> x1, Pallas kernels: none -> 96.3 us  [body(): pl.pallas_call(functools.partial(admm, dims, total), out_shape=(jax.Shape...]
    all_to_all x3 -> x0, blocking collectives: 45.5 us -> none  [from_everyone(): lax.all_to_all(jnp.broadcast_to(value[None], (length, *value.shape)), axi...]
    all_to_all x3 -> x0, waiting for transfers between devices: 35 us -> none  [sent_and_summed(): lax.all_to_all(cut_along(value, dim, length), axis, 0, 0, tiled=True)]
    all_to_all x3 -> x0, starting transfers between devices: 19.8 us -> none  [sent_and_summed(): lax.all_to_all(cut_along(value, dim, length), axis, 0, 0, tiled=True)]
    dot_general x3 -> x0, matrix products: 6.3 us -> none  [iterate(): jnp.dot(kernel, column, preferred_element_type=jnp.float32)]
  transfers between devices with their start and end apart: 6 -> 0, of which waited for: 6 -> 0; matrix products, arithmetic and copies ran while one was open for 0% -> 0% of each run, Pallas kernels for 0% -> 0%
where the time goes in v1:
time: 102 us
  Pallas kernels  96.3 us (94%)
  local copies, waits for them, and re-layouts  5.02 us (5%)
    pallas_call x1, Pallas kernels, body(): pl.pallas_call(functools.partial(admm, dims, total), out_shape=(jax.Shape...  96.3 us
    unnamed x4, local copies, waits for them, and re-layouts  5.02 us

profile of v1, /device:TPU:1, one launch (start us, length us, event | category | flops | bytes accessed | tf_op | source)
XLA Modules:
  0.0 102.0 jit_solution(9656128969165857322)
XLA Ops:
  0.6 96.3 %admm.1 = (f32[40,128]{1,0:T(8,128)}, f32[40,128]{1,0:T(8,128)}, f32[3,128]{1,0:T(4,128)}, f32[1,128]{1,0:T(1,128)}) custom-call(bf16[640,1280]{1,0:T(8,128)(2,1)} %kernel_hbm.1, s32[5,128]{1,0:T(8,128)} %bitcast.4, f32[640,128]{1,0:T(8,128)} %start_hbm.1, f32[1,128]{1,0:T(1,128)} %bitcast.5, f32[1,128]{1,0:T(1,128)} %bitcast.6), custom_call_target="tpu_custom_call" | custom-call | tf_op jit(solution)/shard_map/admm/pallas_call | solution.py:342
  97.0 1.3 %copy.13 = f32[40,128]{1,0:T(8,128)} copy(f32[40,128]{1,0:T(8,128)} %get-tuple-element.16) | data formatting | bytes 40960
  98.3 1.3 %copy.14 = f32[40,128]{1,0:T(8,128)} copy(f32[40,128]{1,0:T(8,128)} %get-tuple-element.17) | data formatting | bytes 40960
  99.6 1.2 %copy.15 = f32[3,128]{1,0:T(4,128)} copy(f32[3,128]{1,0:T(4,128)} %get-tuple-element.18) | data formatting | bytes 3072
  100.9 1.1 %copy.16 = f32[128]{0:T(128)} copy(f32[128]{0:T(128)} %bitcast.7) | data formatting | bytes 1024

commit v2 on v1

v2 whole, which is shorter than its diff:
```python
import functools

import jax
import jax.numpy as jnp
from jax import lax
from jax.experimental import pallas as pl
from jax.experimental.pallas import tpu as pltpu
from jax.sharding import Mesh
from jax.sharding import PartitionSpec as P

ITERS = 3
ROW = ("row_0", "row_1", "row_2")
COL = ("col_0", "col_1")
ROW_COL = ROW + COL
MESH = pl.DeviceIdType.MESH
F32 = jnp.float32
BF16 = jnp.bfloat16


def loop(low, high, step):
    def one(i, carry):
        step(i)
        return carry

    lax.fori_loop(low, high, one, jnp.int32(0))


def spread(count, step):
    def one(j):
        step(count // 2 + lax.div(j + 1, 2) * (2 * lax.rem(j, 2) - 1))

    loop(0, count - 1, one)


def remote(src, dst, send, recv, device):
    return pltpu.make_async_remote_copy(
        src_ref=src, dst_ref=dst, send_sem=send, recv_sem=recv, device_id=device, device_id_type=MESH
    )


def admm(
    dims, total,
    kernel_hbm, labels_hbm, start_hbm, penalty_hbm, box_hbm,
    dual_out, mult_out, gaps_out, offset_out,
    kernel_ref, labels_ref, start_ref, penalty_ref, box_ref, gaps_ref, offset_ref, signs_ref, part_ref, load_sem, store_sem,
    state_send, state_recv, state_ss, state_rs,
    core_send, core_recv, core_ss, core_rs,
    row_send, row_recv, row_ss, row_rs,
    gat_ref, gat_ss, gat_rs, fwd_ss,
    col_send, col_recv, col_ss, col_rs,
    pcol_ref, pcol_ss, pcol_rs,
    near_ref, near_ss, near_rs,
    far_ref, far_ss, far_rs,
    kcore_ref, kx_ref, kh_ref, ksum_ss, ksum_rs, ksum_send, ksum_recv, kmove_sem,
):
    hs, xs, ks, ys, ls = dims
    groups, rows, cols = hs * xs, hs * xs * ks, ys * ls
    h, x, k = (lax.axis_index(a) for a in ROW)
    y, l = (lax.axis_index(a) for a in COL)
    g = h * xs + x
    r = g * ks + k
    c = y * ls + l
    piece = state_send.shape[2]
    near_n, far_n = ys * ks, hs * xs * ls
    near_me = y * ks + k
    far_me = g * ls + l
    other = 1 - k

    def chip(to):
        return {"row_0": lax.div(to, xs), "row_1": lax.rem(to, xs)}

    def column(to):
        return {"col_0": lax.div(to, ls), "col_1": lax.rem(to, ls)}

    def whole(row, col):
        return {
            "row_0": lax.div(row, xs * ks), "row_1": lax.rem(lax.div(row, ks), xs), "row_2": lax.rem(row, ks),
            "col_0": lax.div(col, ls), "col_1": lax.rem(col, ls),
        }

    def near(to):
        return {"col_0": lax.div(to, ks), "row_2": lax.rem(to, ks)}

    def far(to):
        return {
            "row_0": lax.div(to, xs * ls), "row_1": lax.rem(lax.div(to, ls), xs), "col_1": lax.rem(to, ls)
        }

    partner = {"row_2": other}
    mine = g * ks + other
    block = r * cols + c
    to_piece = lax.rem(block, rows)
    to_column = whole(
        lax.div(to_piece, ks) * ks + (ks - 1 - lax.rem(to_piece, ks)), lax.div(block, rows)
    )
    owned = c * rows + mine
    to_row = whole(lax.div(owned, cols), lax.rem(owned, cols))

    load_k = pltpu.make_async_copy(kernel_hbm, kernel_ref, load_sem.at[0])
    load_s = pltpu.make_async_copy(start_hbm, start_ref, load_sem.at[1])
    load_l = pltpu.make_async_copy(labels_hbm, labels_ref, load_sem.at[2])
    load_p = pltpu.make_async_copy(penalty_hbm, penalty_ref, load_sem.at[3])
    load_b = pltpu.make_async_copy(box_hbm, box_ref, load_sem.at[4])
    load_l.start()
    load_b.start()
    load_s.start()
    load_p.start()
    load_k.start()

    barrier = pltpu.get_barrier_semaphore()

    def greet(device):
        pl.semaphore_signal(barrier, inc=1, device_id=device, device_id_type=MESH)

    greet(to_column)
    greet(to_row)
    loop(1, far_n, lambda i: greet(far(lax.rem(far_me + i, far_n))))
    loop(1, near_n, lambda i: greet(near(lax.rem(near_me + i, near_n))))
    crossed = ys * (ls - 1)
    if crossed:
        def cross(i):
            greet({"col_0": lax.rem(i, ys), "col_1": lax.rem(l + 1 + lax.div(i, ys), ls)})
        loop(0, crossed, cross)

    load_l.wait()
    wide = labels_ref.shape[1]
    for i in range(labels_ref.shape[0]):
        line = labels_ref[i : i + 1, :].astype(F32)
        if wide == 128:
            block_signs = jnp.transpose(jnp.broadcast_to(line, (128, 128)))
        else:
            block_signs = jnp.broadcast_to(jnp.transpose(line), (wide, 128))
        signs_ref[i * wide : (i + 1) * wide, :] = block_signs
    load_b.wait()
    load_s.wait()
    load_p.wait()
    penalty = penalty_ref[...]
    box = box_ref[...]
    first = jnp.minimum(jnp.maximum(start_ref[...], 0.0), box)
    start_ref[...] = first
    weighted = (signs_ref[...] * first).astype(BF16)
    own_rows = pl.ds(pl.multiple_of(c * piece, 8), piece)
    signs_row = signs_ref[own_rows, :]
    dual = start_ref[own_rows, :]
    mult = jnp.zeros_like(dual)
    state_send[0, 0] = dual
    state_send[0, 1] = signs_row

    def move_state(t, device):
        remote(state_send.at[t], state_recv.at[t], state_ss.at[t], state_rs.at[t], device).start()

    def arrived_state(t):
        remote(state_send.at[t], state_recv.at[t], state_ss.at[t], state_rs.at[t], to_row).wait_recv()
        return state_recv[t, 0], state_recv[t, 1]

    def near_copy(t, i):
        return remote(near_ref.at[t, near_me], near_ref.at[t, near_me], near_ss.at[t], near_rs.at[t], near(i))

    def near_all(t):
        rest = near_ref.at[t, pl.ds(0, near_n - 1)]
        return remote(rest, rest, near_ss.at[t], near_rs.at[t], partner)

    def far_copy(t, i):
        return remote(far_ref.at[t, far_me], far_ref.at[t, far_me], far_ss.at[t], far_rs.at[t], far(i))

    def far_all(t):
        rest = far_ref.at[t, pl.ds(0, far_n - 1)]
        return remote(rest, rest, far_ss.at[t], far_rs.at[t], partner)

    def sum_start(t, top, bottom):
        near_ref[t, near_me, 0:1, :] = top
        near_ref[t, near_me, 1:2, :] = bottom
        spread(near_n, lambda i: near_copy(t, lax.rem(near_me + i, near_n)).start())

    def sum_middle(t):
        near_all(t).wait_recv()
        far_ref[t, far_me] = jnp.sum(near_ref[t], axis=0)
        spread(far_n, lambda i: far_copy(t, lax.rem(far_me + i, far_n)).start())

    def sum_end(t):
        far_all(t).wait_recv()
        return jnp.sum(far_ref[t], axis=0)

    def ksum_copy(ref, slot, stage, device):
        return remote(ref.at[slot], ref.at[slot], ksum_ss.at[stage], ksum_rs.at[stage], device)

    def ksum_all(ref, stage):
        rest = ref.at[pl.ds(0, ref.shape[0] - 1)]
        return remote(rest, rest, ksum_ss.at[stage], ksum_rs.at[stage], partner)

    def ksum_x():
        ksum_all(kcore_ref, 0).wait_recv()
        kx_ref[x] = jnp.sum(kcore_ref[...], axis=0)
        loop(1, xs, lambda i: ksum_copy(kx_ref, x, 1, {"row_1": lax.rem(x + i, xs)}).start())

    def ksum_h():
        if xs > 1:
            ksum_all(kx_ref, 1).wait_recv()
        kh_ref[h] = jnp.sum(kx_ref[...], axis=0)
        loop(1, hs, lambda i: ksum_copy(kh_ref, h, 2, {"row_0": lax.rem(h + i, hs)}).start())

    def ksum_mine():
        ksum_all(kh_ref, 2).wait_recv()
        sums = jnp.sum(kh_ref[...], axis=0)
        shape = (piece, sums.shape[1])
        here = lax.broadcasted_iota(jnp.int32, shape, 1) == lax.broadcasted_iota(jnp.int32, shape, 0) + mine * piece
        return jnp.sum(jnp.where(here, sums, 0.0), axis=1, keepdims=True)

    def local_bias(dual, mult, signs, product_sum):
        steady = jnp.sum(signs * (dual - mult), axis=0, keepdims=True)
        return steady - (product_sum - jnp.sum(signs, axis=0, keepdims=True)) / penalty

    def update(q, dual, mult, signs, offset):
        w = dual - mult - (q - 1.0) / penalty
        hinge = jnp.maximum(0.0, 1.0 - q - signs * offset)
        gap = jnp.sum(dual * q - dual + box * hinge, axis=0, keepdims=True)
        x_value = w - signs * offset
        dual_next = jnp.minimum(jnp.maximum(x_value + mult, 0.0), box)
        return dual_next, mult + x_value - dual_next, gap

    def row_copy(s, i):
        return remote(row_send.at[s, i], row_recv.at[s, g], row_ss.at[s], row_rs.at[s], chip(i))

    def row_all(s):
        rest = pl.ds(0, groups - 1)
        return remote(row_send.at[s, rest], row_recv.at[s, rest], row_ss.at[s], row_rs.at[s], partner)

    def core_copy(s):
        return remote(core_send.at[s], core_recv.at[s], core_ss.at[s], core_rs.at[s], partner)

    def transposed_start(s, weighted):
        product = lax.dot_general(
            kernel_ref[...], weighted, (((0,), (0,)), ((), ())), preferred_element_type=F32
        )
        part_ref[...] = product.reshape(part_ref.shape)
        core_send[s] = part_ref[:, k].astype(BF16)
        return jnp.sum(product, axis=0, keepdims=True)

    def transposed_send(s):
        core_copy(s).wait_recv()
        both = part_ref[:, other] + core_recv[s].astype(F32)
        part_ref[:, other] = both
        row_send[s] = both.astype(BF16)
        spread(groups, lambda i: row_copy(s, lax.rem(g + i, groups)).start())

    def transposed_sum(s):
        row_recv[s, g] = jnp.zeros(row_recv.shape[2:], BF16)
        row_all(s).wait_recv()
        return part_ref[g, other] + jnp.sum(row_recv[s].astype(F32), axis=0)

    zero = jnp.zeros((1, box.shape[1]), F32)

    load_k.wait()
    product_sum = transposed_start(0, weighted)
    ones = jnp.ones((8, kernel_ref.shape[0]), BF16)
    kcore_ref[k] = jnp.dot(ones, kernel_ref[...], preferred_element_type=F32)[0:1]
    pl.semaphore_wait(barrier, 2 + far_n - 1 + near_n - 1 + crossed)
    core_copy(0).start()
    sum_start(0, local_bias(dual, mult, signs_row, product_sum), zero)
    ksum_copy(kcore_ref, k, 0, partner).start()
    move_state(0, to_column)
    transposed_send(0)
    ksum_x()
    sum_middle(0)
    ksum_h()
    q_sum = transposed_sum(0)
    dual, signs_col = arrived_state(0)
    mult = jnp.zeros_like(dual)
    ksum = ksum_mine()
    offset = sum_end(0)[0:1] / total
    dual, mult, gap = update(signs_col * q_sum, dual, mult, signs_col, offset)

    gat_ref[mine] = (signs_col * dual).astype(BF16)

    def gat_copy(slot, send, device):
        return remote(gat_ref.at[slot], gat_ref.at[slot], send, gat_rs.at[slot], device)

    spread(groups, lambda i: gat_copy(mine, gat_ss.at[0], chip(lax.rem(g + i, groups))).start())
    gat_copy(mine, fwd_ss.at[0], partner).start()
    weighted = gat_ref[mine].astype(F32)
    sum_start(1, local_bias(dual, mult, signs_col, jnp.sum(ksum * weighted, axis=0, keepdims=True)), gap)
    state_send[1, 0] = dual
    state_send[1, 1] = mult
    ksum_send[...] = jnp.broadcast_to(ksum, ksum_send.shape)
    move_state(1, to_row)
    move_ksum = remote(ksum_send, ksum_recv, kmove_sem.at[0], kmove_sem.at[1], to_row)
    move_ksum.start()

    def forward(i):
        slot = lax.rem(g + i, groups) * ks + other
        gat_copy(slot, fwd_ss.at[0], partner).wait_recv()
        gat_copy(slot, fwd_ss.at[0], partner).start()

    loop(1, groups, forward)
    sum_middle(1)
    loop(0, groups, lambda i: gat_copy(i * ks + k, fwd_ss.at[0], partner).wait_recv())
    gathered = gat_ref[...].astype(F32).reshape(rows * piece, -1).astype(BF16)
    product = jnp.dot(kernel_ref[...], gathered, preferred_element_type=F32)
    col_send[...] = product.reshape(col_send.shape).astype(BF16)
    part_ref[0 : cols // ks] = product.reshape(cols // ks, ks, piece, -1)

    def col_copy(i):
        return remote(col_send.at[i], col_recv.at[c], col_ss.at[0], col_rs.at[0], column(i))

    rest = pl.ds(0, cols - 1)
    col_all = remote(col_send.at[rest], col_recv.at[rest], col_ss.at[0], col_rs.at[0], partner)

    spread(cols, lambda i: col_copy(lax.rem(c + i, cols)).start())
    col_recv[c] = jnp.zeros(col_recv.shape[1:], BF16)
    col_all.wait_recv()
    q_sum = part_ref[lax.div(c, ks), lax.rem(c, ks)] + jnp.sum(col_recv[...].astype(F32), axis=0)
    dual, mult = arrived_state(1)
    sums = sum_end(1)
    gaps_ref[0:1, :] = sums[1:2] / total
    offset = sums[0:1] / total
    dual, mult, gap = update(signs_row * q_sum, dual, mult, signs_row, offset)

    pcol_ref[c] = (signs_row * dual).astype(BF16)

    def pcol_copy(i):
        return remote(pcol_ref.at[c], pcol_ref.at[c], pcol_ss.at[0], pcol_rs.at[0], column(i))

    pcol_all = remote(pcol_ref.at[rest], pcol_ref.at[rest], pcol_ss.at[0], pcol_rs.at[0], partner)
    spread(cols, lambda i: pcol_copy(lax.rem(c + i, cols)).start())
    move_ksum.wait_recv()
    weighted = pcol_ref[c].astype(F32)
    sum_start(2, local_bias(dual, mult, signs_row, jnp.sum(ksum_recv[...] * weighted, axis=0, keepdims=True)), gap)
    state_send[2, 0] = dual
    state_send[2, 1] = mult
    move_state(2, to_column)
    pcol_all.wait_recv()
    weighted = pcol_ref[...].astype(F32).reshape(cols * piece, -1).astype(BF16)
    transposed_start(1, weighted)
    core_copy(1).start()
    sum_middle(2)
    transposed_send(1)
    q_sum = transposed_sum(1)
    dual, mult = arrived_state(2)
    sums = sum_end(2)
    gaps_ref[1:2, :] = sums[1:2] / total
    offset = sums[0:1] / total
    dual, mult, gap = update(signs_col * q_sum, dual, mult, signs_col, offset)

    sum_start(3, zero, gap)
    state_send[3, 0] = dual
    state_send[3, 1] = mult
    move_state(3, to_row)
    offset_ref[...] = offset
    store_o = pltpu.make_async_copy(offset_ref, offset_out, store_sem.at[0])
    store_o.start()
    for t in range(3):
        remote(state_send.at[t], state_recv.at[t], state_ss.at[t], state_rs.at[t], to_row).wait_send()
        near_all(t).wait_send()
        far_all(t).wait_send()
    for s in range(2):
        core_copy(s).wait_send()
        row_all(s).wait_send()
    rest = pl.ds(0, groups - 1)
    remote(gat_ref.at[rest], gat_ref.at[rest], gat_ss.at[0], gat_rs.at[0], partner).wait_send()
    rest = pl.ds(0, groups)
    remote(gat_ref.at[rest], gat_ref.at[rest], fwd_ss.at[0], gat_rs.at[0], partner).wait_send()
    col_all.wait_send()
    pcol_all.wait_send()
    move_ksum.wait_send()
    ksum_all(kcore_ref, 0).wait_send()
    if xs > 1:
        ksum_all(kx_ref, 1).wait_send()
    ksum_all(kh_ref, 2).wait_send()
    sum_middle(3)
    remote(state_send.at[3], state_recv.at[3], state_ss.at[3], state_rs.at[3], to_row).wait()
    store_d = pltpu.make_async_copy(state_recv.at[3, 0], dual_out, store_sem.at[1])
    store_m = pltpu.make_async_copy(state_recv.at[3, 1], mult_out, store_sem.at[2])
    store_d.start()
    store_m.start()
    gaps_ref[2:3, :] = sum_end(3)[1:2] / total
    store_g = pltpu.make_async_copy(gaps_ref, gaps_out, store_sem.at[3])
    store_g.start()
    near_all(3).wait_send()
    far_all(3).wait_send()
    store_o.wait()
    store_d.wait()
    store_m.wait()
    store_g.wait()


def hand_over(*refs):
    half = len(refs) // 2
    for source, target in zip(refs[:half], refs[half:]):
        target[...] = source[...]


def body(dims, kernel, labels, start_dual, penalty, box):
    hs, xs, ks, ys, ls = dims
    groups, rows, cols = hs * xs, hs * xs * ks, ys * ls
    height, width = kernel.shape
    settings = box.shape[0]
    piece = height // cols
    total = height * rows
    near_n, far_n = ys * ks, hs * xs * ls
    wide = 128 if height % 128 == 0 else height
    dma = pltpu.SemaphoreType.DMA
    vmem = pltpu.VMEM
    scratch = [
        vmem((height, width), BF16), vmem((height // wide, wide), jnp.int32), vmem((height, settings), F32),
        vmem((1, settings), F32), vmem((1, settings), F32), vmem((ITERS, settings), F32), vmem((1, settings), F32),
        vmem((height, settings), F32), vmem((groups, ks, piece, settings), F32), dma((5,)), dma((4,)),
        vmem((4, 2, piece, settings), F32), vmem((4, 2, piece, settings), F32), dma((4,)), dma((4,)),
        vmem((2, groups, piece, settings), BF16), vmem((2, groups, piece, settings), BF16), dma((2,)), dma((2,)),
        vmem((2, groups, piece, settings), BF16), vmem((2, groups, piece, settings), BF16), dma((2,)), dma((2,)),
        vmem((rows, piece, settings), BF16), dma((1,)), dma((rows,)), dma((1,)),
        vmem((cols, piece, settings), BF16), vmem((cols, piece, settings), BF16), dma((1,)), dma((1,)),
        vmem((cols, piece, settings), BF16), dma((1,)), dma((1,)),
        vmem((4, near_n, 2, settings), F32), dma((4,)), dma((4,)),
        vmem((4, far_n, 2, settings), F32), dma((4,)), dma((4,)),
        vmem((ks, 1, width), F32), vmem((xs, 1, width), F32), vmem((hs, 1, width), F32), dma((3,)), dma((3,)),
        vmem((piece, settings), F32), vmem((piece, settings), F32), dma((2,)),
    ]
    in_vmem = pl.BlockSpec(memory_space=vmem)
    in_hbm = pl.BlockSpec(memory_space=pltpu.HBM)
    outs_shape = tuple(
        jax.ShapeDtypeStruct(shape, F32)
        for shape in ((piece, settings), (piece, settings), (ITERS, settings), (1, settings))
    )
    outs = pl.pallas_call(
        functools.partial(admm, dims, total),
        out_shape=outs_shape,
        in_specs=[in_hbm] * 5,
        out_specs=(in_hbm,) * 4,
        scratch_shapes=scratch,
        compiler_params=pltpu.CompilerParams(collective_id=0, has_side_effects=True),
        name="admm",
    )(kernel, labels.reshape(height // wide, wide), start_dual, penalty[None, :], box[None, :])
    dual, mult, gaps, offset = pl.pallas_call(
        hand_over, out_shape=outs_shape, in_specs=[in_vmem] * 4, out_specs=(in_vmem,) * 4, name="hand_over"
    )(*outs)
    return dual, mult, gaps, offset[0]


def build(torus):
    dims = torus.devices.shape
    in_specs = (P(ROW, COL), P(ROW), P(ROW, None), P(), P())
    out_specs = (P(ROW_COL, None), P(ROW_COL, None), P(), P())
    return jax.shard_map(
        functools.partial(body, dims), mesh=torus, in_specs=in_specs, out_specs=out_specs, check_vma=False
    )


def solution(mesh):
    return build(Mesh(mesh.devices.reshape(4, 4, 2, 8, 2), ROW_COL))
```

time: 102 us -> 86.1 us (0.84)
  Pallas kernels: 96.3 us -> 85.2 us
  local copies, waits for them, and re-layouts: 5.02 us -> 0 us
    pallas_call x1 -> x2, Pallas kernels: 96.3 us -> 85.2 us  [the longest x1 83.8 us: body(): pl.pallas_call(functools.partial(admm, dims, total), out_shape=outs_shape...]
    unnamed x4 -> x0, local copies, waits for them, and re-layouts: 5.02 us -> none
where the time goes in v2:
time: 86.1 us; the launch traced here: 85.9 us
  Pallas kernels  85.2 us (99%)
    pallas_call x1, Pallas kernels, body(): pl.pallas_call(functools.partial(admm, dims, total), out_shape=outs_shape...  83.8 us

profile of v2, /device:TPU:1, one launch (start us, length us, event | category | flops | bytes accessed | tf_op | source)
XLA Modules:
  0.0 85.9 jit_solution(2676342536793945735)
XLA Ops:
  0.6 83.8 %admm.1 = (f32[40,128]{1,0:T(8,128)}, f32[40,128]{1,0:T(8,128)}, f32[3,128]{1,0:T(4,128)}, f32[1,128]{1,0:T(1,128)}) custom-call(bf16[640,1280]{1,0:T(8,128)(2,1)} %kernel_hbm.1, s32[5,128]{1,0:T(8,128)} %bitcast.4, f32[640,128]{1,0:T(8,128)} %start_hbm.1, f32[1,128]{1,0:T(1,128)} %bitcast.5, f32[1,128]{1,0:T(1,128)} %bitcast.6), custom_call_target="tpu_custom_call" | custom-call | tf_op jit(solution)/shard_map/admm/pallas_call | solution.py:424
  84.5 1.4 %hand_over.1 = (f32[40,128]{1,0:T(8,128)}, f32[40,128]{1,0:T(8,128)}, f32[3,128]{1,0:T(4,128)}, f32[1,128]{1,0:T(1,128)}) custom-call(f32[40,128]{1,0:T(8,128)} %get-tuple-element.12.refs_0_, f32[40,128]{1,0:T(8,128)} %get-tuple-element.13.refs_1_, f32[3,128]{1,0:T(4,128)} %get-tuple-element.14.refs_2_, f32[1,128]{1,0:T(1,128)} %get-tuple-element.15.refs_3_), custom_call_target="tpu_custom_call" | custom-call | tf_op jit(solution)/shard_map/hand_over/pallas_call | solution.py:433

commit v3 on v2

v3 whole, which is shorter than its diff:
```python
import functools

import jax
import jax.numpy as jnp
from jax import lax
from jax.experimental import pallas as pl
from jax.experimental.pallas import tpu as pltpu
from jax.sharding import Mesh
from jax.sharding import PartitionSpec as P

ITERS = 3
ROW = ("row_0", "row_1", "row_2")
COL = ("col_0", "col_1")
ROW_COL = ROW + COL
MESH = pl.DeviceIdType.MESH
F32 = jnp.float32
BF16 = jnp.bfloat16
I16 = jnp.int16
LEVELS = 32767.0


def loop(low, high, step):
    def one(i, carry):
        step(i)
        return carry

    lax.fori_loop(low, high, one, jnp.int32(0))


def spread(count, step):
    def one(j):
        step(count // 2 + lax.div(j + 1, 2) * (2 * lax.rem(j, 2) - 1))

    loop(0, count - 1, one)


def flip(i):
    return i + 1 - 2 * lax.rem(i, 2)


def coded(values):
    most = jnp.maximum(jnp.max(jnp.max(jnp.abs(values), axis=0), axis=0, keepdims=True), 1e-30)
    return jnp.round(values * (LEVELS / most)).astype(jnp.int32).astype(I16), most / LEVELS


def decoded_sum(codes, scales):
    return jnp.sum(codes.astype(jnp.int32).astype(F32) * scales, axis=0)


def write_signs(labels_ref, signs_ref):
    wide = labels_ref.shape[1]
    for i in range(labels_ref.shape[0]):
        line = labels_ref[i : i + 1, :].astype(F32)
        if wide == 128:
            block_signs = jnp.transpose(jnp.broadcast_to(line, (128, 128)))
        else:
            block_signs = jnp.broadcast_to(jnp.transpose(line), (wide, 128))
        signs_ref[i * wide : (i + 1) * wide, :] = block_signs


def remote(src, dst, send, recv, device):
    return pltpu.make_async_remote_copy(
        src_ref=src, dst_ref=dst, send_sem=send, recv_sem=recv, device_id=device, device_id_type=MESH
    )


def admm(
    dims, total,
    kernel_hbm, labels_hbm, start_hbm, penalty_hbm, box_hbm,
    dual_out, mult_out, gaps_out, offset_out,
    kernel_ref, labels_ref, start_ref, penalty_ref, box_ref, dual_ref, mult_ref, gaps_ref, offset_ref, signs_ref, part_ref,
    load_sem, store_sem,
    first_ref, first_labels_ref, first_signs_ref, first_ss, first_rs,
    state_send, state_recv, state_ss, state_rs,
    core_recv, core_ss, core_rs,
    row_send, row_recv, row_ss, row_rs, rscale_send, rscale_recv, rscale_ss, rscale_rs,
    gat_ref, gat_ss, gat_rs, fwd_ss,
    col_send, col_recv, col_ss, col_rs, cscale_send, cscale_recv, cscale_ss, cscale_rs,
    pcol_ref, pcol_ss, pcol_rs,
    near_ref, near_ss, near_rs,
    far_ref, far_ss, far_rs,
    kcore_ref, kx_ref, kh_ref, ksum_ss, ksum_rs, ksum_send, ksum_recv, kmove_sem,
):
    hs, xs, ks, ys, ls = dims
    groups, rows, cols = hs * xs, hs * xs * ks, ys * ls
    h, x, k = (lax.axis_index(a) for a in ROW)
    y, l = (lax.axis_index(a) for a in COL)
    g = h * xs + x
    r = g * ks + k
    c = y * ls + l
    piece, settings = state_send.shape[1:]
    half = groups * piece
    near_n, far_n = ys * ks, hs * xs * ls
    near_me = y * ks + k
    far_me = g * ls + l
    other = 1 - k

    def chip(to):
        return {"row_0": lax.div(to, xs), "row_1": lax.rem(to, xs)}

    def column(to):
        return {"col_0": lax.div(to, ls), "col_1": lax.rem(to, ls)}

    def whole(row, col):
        return {
            "row_0": lax.div(row, xs * ks), "row_1": lax.rem(lax.div(row, ks), xs), "row_2": lax.rem(row, ks),
            "col_0": lax.div(col, ls), "col_1": lax.rem(col, ls),
        }

    def near(to):
        return {"col_0": lax.div(to, ks), "row_2": lax.rem(to, ks)}

    def far(to):
        return {
            "row_0": lax.div(to, xs * ls), "row_1": lax.rem(lax.div(to, ls), xs), "col_1": lax.rem(to, ls)
        }

    partner = {"row_2": other}
    spot = flip(g)
    mine = k * groups + spot
    block = r * cols + c
    to_piece = lax.rem(block, rows)
    to_column = whole(
        flip(lax.rem(to_piece, groups)) * ks + lax.div(to_piece, groups), lax.div(block, rows)
    )
    owned = c * rows + mine
    to_row = whole(lax.div(owned, cols), lax.rem(owned, cols))

    load_k = pltpu.make_async_copy(kernel_hbm, kernel_ref, load_sem.at[0])
    load_s = pltpu.make_async_copy(start_hbm, start_ref, load_sem.at[1])
    load_l = pltpu.make_async_copy(labels_hbm, labels_ref, load_sem.at[2])
    load_p = pltpu.make_async_copy(penalty_hbm, penalty_ref, load_sem.at[3])
    load_b = pltpu.make_async_copy(box_hbm, box_ref, load_sem.at[4])
    load_l.start()
    load_b.start()
    load_s.start()
    load_p.start()
    load_k.start()

    barrier = pltpu.get_barrier_semaphore()

    def greet(device):
        pl.semaphore_signal(barrier, inc=1, device_id=device, device_id_type=MESH)

    loop(1, far_n, lambda i: greet(far(lax.rem(far_me + i, far_n))))
    loop(1, near_n, lambda i: greet(near(lax.rem(near_me + i, near_n))))
    crossed = ys * (ls - 1)
    if crossed:
        def cross(i):
            greet({"col_0": lax.rem(i, ys), "col_1": lax.rem(l + 1 + lax.div(i, ys), ls)})
        loop(0, crossed, cross)

    load_l.wait()
    write_signs(labels_ref, signs_ref)
    load_b.wait()
    load_s.wait()
    load_p.wait()
    penalty = penalty_ref[...]
    box = box_ref[...]
    def clipped(values):
        return jnp.minimum(jnp.maximum(values, 0.0), box)

    weighted = (signs_ref[...] * clipped(start_ref[...])).astype(BF16)
    own_rows = pl.ds(pl.multiple_of(c * piece, 8), piece)
    signs_row = signs_ref[own_rows, :]
    dual = clipped(start_ref[own_rows, :])
    mult = jnp.zeros_like(dual)

    from_here = lax.div(g, ls) == y
    to_side = lax.rem(g, ls)
    local = jnp.logical_and(g == c, lax.rem(spot, ls) == l)

    def first_copies(j, device):
        rows_j = pl.ds(pl.multiple_of(j * piece, 8), piece)
        return (
            remote(start_ref.at[rows_j], first_ref, first_ss.at[0, lax.div(j, ls)], first_rs.at[0], device),
            remote(labels_ref, first_labels_ref, first_ss.at[1, lax.div(j, ls)], first_rs.at[1], device),
        )

    def first_each(act):
        def one(i):
            j = i * ls + l
            to = flip(j)

            @pl.when(jnp.logical_not(jnp.logical_and(to == g, to_side == l)))
            def _():
                device = {"row_0": lax.div(to, xs), "row_1": lax.rem(to, xs), "col_1": to_side}
                for copy in first_copies(j, device):
                    act(copy)

        @pl.when(from_here)
        def _():
            loop(0, groups // ls, one)

    def first_arrived():
        @pl.when(jnp.logical_not(local))
        def _():
            for copy in first_copies(0, partner):
                copy.wait_recv()

        @pl.when(local)
        def _():
            first_ref[...] = start_ref[pl.ds(pl.multiple_of(spot * piece, 8), piece), :]
            first_labels_ref[...] = labels_ref[...]

        write_signs(first_labels_ref, first_signs_ref)
        return clipped(first_ref[...]), first_signs_ref[pl.ds(pl.multiple_of(spot * piece, 8), piece), :]

    def state_copy(t, device):
        return remote(state_send.at[t], state_recv.at[t], state_ss.at[t], state_rs.at[t], device)

    def move_state(t, state, device):
        state_send[t] = state
        state_copy(t, device).start()

    def arrived_state(t):
        state_copy(t, to_row).wait_recv()
        state = state_recv[t]
        return clipped(state), state - clipped(state)

    def near_copy(t, i):
        return remote(near_ref.at[t, near_me], near_ref.at[t, near_me], near_ss.at[t], near_rs.at[t], near(i))

    def near_all(t):
        rest = near_ref.at[t, pl.ds(0, near_n - 1)]
        return remote(rest, rest, near_ss.at[t], near_rs.at[t], partner)

    def far_copy(t, i):
        return remote(far_ref.at[t, far_me], far_ref.at[t, far_me], far_ss.at[t], far_rs.at[t], far(i))

    def far_all(t):
        rest = far_ref.at[t, pl.ds(0, far_n - 1)]
        return remote(rest, rest, far_ss.at[t], far_rs.at[t], partner)

    def sum_start(t, top, bottom):
        near_ref[t, near_me, 0:1, :] = top
        near_ref[t, near_me, 1:2, :] = bottom
        spread(near_n, lambda i: near_copy(t, lax.rem(near_me + i, near_n)).start())

    def sum_middle(t):
        near_all(t).wait_recv()
        far_ref[t, far_me] = jnp.sum(near_ref[t], axis=0)
        spread(far_n, lambda i: far_copy(t, lax.rem(far_me + i, far_n)).start())

    def sum_end(t):
        far_all(t).wait_recv()
        return jnp.sum(far_ref[t], axis=0)

    def ksum_copy(ref, slot, stage, device):
        return remote(ref.at[slot], ref.at[slot], ksum_ss.at[stage], ksum_rs.at[stage], device)

    def ksum_all(ref, stage):
        rest = ref.at[pl.ds(0, ref.shape[0] - 1)]
        return remote(rest, rest, ksum_ss.at[stage], ksum_rs.at[stage], partner)

    def ksum_x():
        ksum_all(kcore_ref, 0).wait_recv()
        kx_ref[x] = jnp.sum(kcore_ref[...], axis=0)
        loop(1, xs, lambda i: ksum_copy(kx_ref, x, 1, {"row_1": lax.rem(x + i, xs)}).start())

    def ksum_h():
        if xs > 1:
            ksum_all(kx_ref, 1).wait_recv()
        kh_ref[h] = jnp.sum(kx_ref[...], axis=0)
        loop(1, hs, lambda i: ksum_copy(kh_ref, h, 2, {"row_0": lax.rem(h + i, hs)}).start())

    def ksum_row():
        ksum_all(kh_ref, 2).wait_recv()
        return jnp.sum(kh_ref[...], axis=0)

    def ksum_of(sums, at):
        shape = (piece, sums.shape[1])
        here = lax.broadcasted_iota(jnp.int32, shape, 1) == lax.broadcasted_iota(jnp.int32, shape, 0) + at * piece
        return jnp.sum(jnp.where(here, sums, 0.0), axis=1, keepdims=True)

    def local_bias(dual, mult, signs, product_sum):
        steady = jnp.sum(signs * (dual - mult), axis=0, keepdims=True)
        return steady - (product_sum - jnp.sum(signs, axis=0, keepdims=True)) / penalty

    def update(q, dual, mult, signs, offset):
        w = dual - mult - (q - 1.0) / penalty
        hinge = jnp.maximum(0.0, 1.0 - q - signs * offset)
        gap = jnp.sum(dual * q - dual + box * hinge, axis=0, keepdims=True)
        x_value = w - signs * offset
        state = x_value + mult
        return state, clipped(state), state - clipped(state), gap

    def row_copies(s, i):
        j = flip(i)
        return (
            remote(row_send.at[s, j], row_recv.at[s, g], row_ss.at[s], row_rs.at[s], chip(i)),
            remote(rscale_send.at[s], rscale_recv.at[s, g], rscale_ss.at[s], rscale_rs.at[s], chip(i)),
        )

    def row_all(s):
        rest = pl.ds(0, groups - 1)
        return (
            remote(row_send.at[s, rest], row_recv.at[s, rest], row_ss.at[s], row_rs.at[s], partner),
            remote(rscale_recv.at[s, rest], rscale_recv.at[s, rest], rscale_ss.at[s], rscale_rs.at[s], partner),
        )

    def core_copy(s):
        return remote(part_ref.at[other], core_recv.at[s], core_ss.at[s], core_rs.at[s], partner)

    def transposed_half(which, weighted):
        columns = pl.ds(pl.multiple_of(which * half, 128) if half % 128 == 0 else which * half, half)
        product = lax.dot_general(
            kernel_ref[:, columns], weighted, (((0,), (0,)), ((), ())), preferred_element_type=F32
        )
        part_ref[which] = product.reshape(part_ref.shape[1:])
        return jnp.sum(product, axis=0, keepdims=True)

    def transposed_send(s):
        core_copy(s).wait_recv()
        both = part_ref[k] + core_recv[s]
        part_ref[k] = both
        row_send[s], rscale_send[s] = coded(both)

        def send(i):
            for copy in row_copies(s, lax.rem(g + i, groups)):
                copy.start()

        spread(groups, send)

    def transposed_sum(s):
        row_recv[s, g] = jnp.zeros(row_recv.shape[2:], I16)
        rscale_recv[s, g] = jnp.zeros(rscale_recv.shape[2:], F32)
        for copy in row_all(s):
            copy.wait_recv()
        return part_ref[k, spot] + decoded_sum(row_recv[s], rscale_recv[s])

    zero = jnp.zeros((1, box.shape[1]), F32)

    load_k.wait()
    far_sum = transposed_half(other, weighted)
    pl.semaphore_wait(barrier, far_n - 1 + near_n - 1 + crossed)
    core_copy(0).start()
    product_sum = far_sum + transposed_half(k, weighted)
    ones = jnp.ones((8, kernel_ref.shape[0]), BF16)
    kcore_ref[k] = jnp.dot(ones, kernel_ref[...], preferred_element_type=F32)[0:1]
    sum_start(0, local_bias(dual, mult, signs_row, product_sum), zero)
    ksum_copy(kcore_ref, k, 0, partner).start()
    transposed_send(0)
    first_each(lambda copy: copy.start())
    ksum_x()
    sum_middle(0)
    ksum_h()
    q_sum = transposed_sum(0)
    core_copy(0).wait_send()
    dual, signs_col = first_arrived()
    mult = jnp.zeros_like(dual)
    ksum_send[...] = ksum_row()
    ksum = ksum_of(ksum_send[...], mine)
    offset = sum_end(0)[0:1] / total
    state, dual, mult, gap = update(signs_col * q_sum, dual, mult, signs_col, offset)

    gat_ref[mine] = (signs_col * dual).astype(BF16)

    def gat_copy(slot, send, device):
        return remote(gat_ref.at[slot], gat_ref.at[slot], send, gat_rs.at[slot], device)

    spread(groups, lambda i: gat_copy(mine, gat_ss.at[0], chip(lax.rem(g + i, groups))).start())
    gat_copy(mine, fwd_ss.at[0], partner).start()
    weighted = gat_ref[mine].astype(F32)
    sum_start(1, local_bias(dual, mult, signs_col, jnp.sum(ksum * weighted, axis=0, keepdims=True)), gap)
    move_state(0, state, to_row)
    move_ksum = remote(ksum_send, ksum_recv, kmove_sem.at[0], kmove_sem.at[1], to_row)
    move_ksum.start()

    def forward(i):
        slot = k * groups + flip(lax.rem(g + i, groups))
        gat_copy(slot, fwd_ss.at[0], partner).wait_recv()
        gat_copy(slot, fwd_ss.at[0], partner).start()

    loop(1, groups, forward)
    sum_middle(1)
    loop(0, groups, lambda i: gat_copy(other * groups + i, fwd_ss.at[0], partner).wait_recv())
    gathered = gat_ref[...].astype(F32).reshape(rows * piece, -1).astype(BF16)
    product = jnp.dot(kernel_ref[...], gathered, preferred_element_type=F32)
    product = product.reshape(cols, piece, settings)
    col_send[...], cscale_send[...] = coded(product)
    part_ref[0] = product

    def col_copies(i):
        return (
            remote(col_send.at[i], col_recv.at[c], col_ss.at[0], col_rs.at[0], column(i)),
            remote(cscale_send, cscale_recv.at[c], cscale_ss.at[0], cscale_rs.at[0], column(i)),
        )

    def col_start(i):
        for copy in col_copies(lax.rem(c + i, cols)):
            copy.start()

    rest = pl.ds(0, cols - 1)
    col_all = (
        remote(col_send.at[rest], col_recv.at[rest], col_ss.at[0], col_rs.at[0], partner),
        remote(cscale_recv.at[rest], cscale_recv.at[rest], cscale_ss.at[0], cscale_rs.at[0], partner),
    )

    spread(cols, col_start)
    col_recv[c] = jnp.zeros(col_recv.shape[1:], I16)
    cscale_recv[c] = jnp.zeros(cscale_recv.shape[1:], F32)
    for copy in col_all:
        copy.wait_recv()
    q_sum = part_ref[0, c] + decoded_sum(col_recv[...], cscale_recv[...])
    dual, mult = arrived_state(0)
    sums = sum_end(1)
    gaps_ref[0:1, :] = sums[1:2] / total
    offset = sums[0:1] / total
    state, dual, mult, gap = update(signs_row * q_sum, dual, mult, signs_row, offset)

    pcol_ref[c] = (signs_row * dual).astype(BF16)

    def pcol_copy(i):
        return remote(pcol_ref.at[c], pcol_ref.at[c], pcol_ss.at[0], pcol_rs.at[0], column(i))

    pcol_all = remote(pcol_ref.at[rest], pcol_ref.at[rest], pcol_ss.at[0], pcol_rs.at[0], partner)
    spread(cols, lambda i: pcol_copy(lax.rem(c + i, cols)).start())
    move_ksum.wait_recv()
    weighted = pcol_ref[c].astype(F32)
    ksum = ksum_of(ksum_recv[...], lax.rem(block, rows))
    sum_start(2, local_bias(dual, mult, signs_row, jnp.sum(ksum * weighted, axis=0, keepdims=True)), gap)
    move_state(1, state, to_column)
    pcol_all.wait_recv()
    weighted = pcol_ref[...].astype(F32).reshape(cols * piece, -1).astype(BF16)
    transposed_half(other, weighted)
    core_copy(1).start()
    transposed_half(k, weighted)
    sum_middle(2)
    transposed_send(1)
    q_sum = transposed_sum(1)
    dual, mult = arrived_state(1)
    sums = sum_end(2)
    gaps_ref[1:2, :] = sums[1:2] / total
    offset = sums[0:1] / total
    state, dual, mult, gap = update(signs_col * q_sum, dual, mult, signs_col, offset)

    sum_start(3, zero, gap)
    move_state(2, state, to_row)
    offset_ref[...] = offset
    store_o = pltpu.make_async_copy(offset_ref, offset_out, store_sem.at[0])
    store_o.start()
    for t in range(3):
        near_all(t).wait_send()
        far_all(t).wait_send()
    state_copy(0, to_row).wait_send()
    state_copy(1, to_row).wait_send()
    core_copy(1).wait_send()
    for copy in row_all(0) + row_all(1) + col_all:
        copy.wait_send()
    first_each(lambda copy: copy.wait_send())
    rest = pl.ds(0, groups - 1)
    remote(gat_ref.at[rest], gat_ref.at[rest], gat_ss.at[0], gat_rs.at[0], partner).wait_send()
    rest = pl.ds(0, groups)
    remote(gat_ref.at[rest], gat_ref.at[rest], fwd_ss.at[0], gat_rs.at[0], partner).wait_send()
    pcol_all.wait_send()
    move_ksum.wait_send()
    ksum_all(kcore_ref, 0).wait_send()
    if xs > 1:
        ksum_all(kx_ref, 1).wait_send()
    ksum_all(kh_ref, 2).wait_send()
    sum_middle(3)
    state_copy(2, to_row).wait_send()
    dual_ref[...], mult_ref[...] = arrived_state(2)
    store_d = pltpu.make_async_copy(dual_ref, dual_out, store_sem.at[1])
    store_m = pltpu.make_async_copy(mult_ref, mult_out, store_sem.at[2])
    store_d.start()
    store_m.start()
    gaps_ref[2:3, :] = sum_end(3)[1:2] / total
    store_g = pltpu.make_async_copy(gaps_ref, gaps_out, store_sem.at[3])
    store_g.start()
    near_all(3).wait_send()
    far_all(3).wait_send()
    store_o.wait()
    store_d.wait()
    store_m.wait()
    store_g.wait()


def hand_over(*refs):
    half = len(refs) // 2
    for source, target in zip(refs[:half], refs[half:]):
        target[...] = source[...]


def body(dims, kernel, labels, start_dual, penalty, box):
    hs, xs, ks, ys, ls = dims
    groups, rows, cols = hs * xs, hs * xs * ks, ys * ls
    height, width = kernel.shape
    settings = box.shape[0]
    piece = height // cols
    total = height * rows
    near_n, far_n = ys * ks, hs * xs * ls
    wide = 128 if height % 128 == 0 else height
    dma = pltpu.SemaphoreType.DMA
    vmem = pltpu.VMEM
    scratch = [
        vmem((height, width), BF16), vmem((height // wide, wide), jnp.int32), vmem((height, settings), F32),
        vmem((1, settings), F32), vmem((1, settings), F32), vmem((piece, settings), F32), vmem((piece, settings), F32),
        vmem((ITERS, settings), F32), vmem((1, settings), F32), vmem((height, settings), F32),
        vmem((ks, groups, piece, settings), F32), dma((5,)), dma((4,)),
        vmem((piece, settings), F32), vmem((height // wide, wide), jnp.int32), vmem((height, settings), F32), dma((2, groups // ls)), dma((2,)),
        vmem((3, piece, settings), F32), vmem((3, piece, settings), F32), dma((3,)), dma((3,)),
        vmem((2, groups, piece, settings), F32), dma((2,)), dma((2,)),
        vmem((2, groups, piece, settings), I16), vmem((2, groups, piece, settings), I16), dma((2,)), dma((2,)),
        vmem((2, 1, settings), F32), vmem((2, groups, 1, settings), F32), dma((2,)), dma((2,)),
        vmem((rows, piece, settings), BF16), dma((1,)), dma((rows,)), dma((1,)),
        vmem((cols, piece, settings), I16), vmem((cols, piece, settings), I16), dma((1,)), dma((1,)),
        vmem((1, settings), F32), vmem((cols, 1, settings), F32), dma((1,)), dma((1,)),
        vmem((cols, piece, settings), BF16), dma((1,)), dma((1,)),
        vmem((4, near_n, 2, settings), F32), dma((4,)), dma((4,)),
        vmem((4, far_n, 2, settings), F32), dma((4,)), dma((4,)),
        vmem((ks, 1, width), F32), vmem((xs, 1, width), F32), vmem((hs, 1, width), F32), dma((3,)), dma((3,)),
        vmem((1, width), F32), vmem((1, width), F32), dma((2,)),
    ]
    in_vmem = pl.BlockSpec(memory_space=vmem)
    in_hbm = pl.BlockSpec(memory_space=pltpu.HBM)
    outs_shape = tuple(
        jax.ShapeDtypeStruct(shape, F32)
        for shape in ((piece, settings), (piece, settings), (ITERS, settings), (1, settings))
    )
    outs = pl.pallas_call(
        functools.partial(admm, dims, total),
        out_shape=outs_shape,
        in_specs=[in_hbm] * 5,
        out_specs=(in_hbm,) * 4,
        scratch_shapes=scratch,
        compiler_params=pltpu.CompilerParams(collective_id=0, has_side_effects=True),
        name="admm",
    )(kernel, labels.reshape(height // wide, wide), start_dual, penalty[None, :], box[None, :])
    dual, mult, gaps, offset = pl.pallas_call(
        hand_over, out_shape=outs_shape, in_specs=[in_vmem] * 4, out_specs=(in_vmem,) * 4, name="hand_over"
    )(*outs)
    return dual, mult, gaps, offset[0]


def build(torus):
    dims = torus.devices.shape
    in_specs = (P(ROW, COL), P(ROW), P(ROW, None), P(), P())
    out_specs = (P(ROW_COL, None), P(ROW_COL, None), P(), P())
    return jax.shard_map(
        functools.partial(body, dims), mesh=torus, in_specs=in_specs, out_specs=out_specs, check_vma=False
    )


def solution(mesh):
    return build(Mesh(mesh.devices.reshape(4, 4, 2, 8, 2), ROW_COL))
```

time: 86.1 us -> 78.3 us (0.909)
  Pallas kernels: 85.2 us -> 77.5 us
    pallas_call x1, Pallas kernels: 83.8 us -> 76.1 us  [body(): pl.pallas_call(functools.partial(admm, dims, total), out_shape=outs_shape...]
where the time goes in v3:
time: 78.3 us; the launch traced here: 78.1 us
  Pallas kernels  77.5 us (99%)
    pallas_call x1, Pallas kernels, body(): pl.pallas_call(functools.partial(admm, dims, total), out_shape=outs_shape...  76.1 us

profile of v3, /device:TPU:1, one launch (start us, length us, event | category | flops | bytes accessed | tf_op | source)
XLA Modules:
  0.0 78.1 jit_solution(73696289381469046)
XLA Ops:
  0.6 76.1 %admm.1 = (f32[40,128]{1,0:T(8,128)}, f32[40,128]{1,0:T(8,128)}, f32[3,128]{1,0:T(4,128)}, f32[1,128]{1,0:T(1,128)}) custom-call(bf16[640,1280]{1,0:T(8,128)(2,1)} %kernel_hbm.1, s32[5,128]{1,0:T(8,128)} %bitcast.4, f32[640,128]{1,0:T(8,128)} %start_hbm.1, f32[1,128]{1,0:T(1,128)} %bitcast.5, f32[1,128]{1,0:T(1,128)} %bitcast.6), custom_call_target="tpu_custom_call" | custom-call | tf_op jit(solution)/shard_map/admm/pallas_call | solution.py:522
  76.8 1.4 %hand_over.1 = (f32[40,128]{1,0:T(8,128)}, f32[40,128]{1,0:T(8,128)}, f32[3,128]{1,0:T(4,128)}, f32[1,128]{1,0:T(1,128)}) custom-call(f32[40,128]{1,0:T(8,128)} %get-tuple-element.12.refs_0_, f32[40,128]{1,0:T(8,128)} %get-tuple-element.13.refs_1_, f32[3,128]{1,0:T(4,128)} %get-tuple-element.14.refs_2_, f32[1,128]{1,0:T(1,128)} %get-tuple-element.15.refs_3_), custom_call_target="tpu_custom_call" | custom-call | tf_op jit(solution)/shard_map/hand_over/pallas_call | solution.py:531

commit v4 on v3

--- a/solution.py
+++ b/solution.py
@@ -68,8 +68,8 @@
     dims, total,
     kernel_hbm, labels_hbm, start_hbm, penalty_hbm, box_hbm,
     dual_out, mult_out, gaps_out, offset_out,
-    kernel_ref, labels_ref, start_ref, penalty_ref, box_ref, dual_ref, mult_ref, gaps_ref, offset_ref, signs_ref, part_ref,
-    load_sem, store_sem,
+    kernel_ref, turned_ref, weighted_ref, labels_ref, start_ref, penalty_ref, box_ref, signs_ref, part_ref,
+    load_sem,
     first_ref, first_labels_ref, first_signs_ref, first_ss, first_rs,
     state_send, state_recv, state_ss, state_rs,
     core_recv, core_ss, core_rs,
@@ -91,8 +91,8 @@
     piece, settings = state_send.shape[1:]
     half = groups * piece
     near_n, far_n = ys * ks, hs * xs * ls
-    near_me = y * ks + k
-    far_me = g * ls + l
+    near_me = k * ys + y
+    far_me = l * groups + g
     other = 1 - k
 
     def chip(to):
@@ -108,12 +108,11 @@
         }
 
     def near(to):
-        return {"col_0": lax.div(to, ks), "row_2": lax.rem(to, ks)}
+        return {"row_2": lax.div(to, ys), "col_0": lax.rem(to, ys)}
 
     def far(to):
-        return {
-            "row_0": lax.div(to, xs * ls), "row_1": lax.rem(lax.div(to, ls), xs), "col_1": lax.rem(to, ls)
-        }
+        on = lax.rem(to, groups)
+        return {"row_0": lax.div(on, xs), "row_1": lax.rem(on, xs), "col_1": lax.div(to, groups)}
 
     partner = {"row_2": other}
     spot = flip(g)
@@ -142,7 +141,7 @@
     def greet(device):
         pl.semaphore_signal(barrier, inc=1, device_id=device, device_id_type=MESH)
 
-    loop(1, far_n, lambda i: greet(far(lax.rem(far_me + i, far_n))))
+    spread(far_n, lambda i: greet(far(lax.rem(far_me + i, far_n))))
     loop(1, near_n, lambda i: greet(near(lax.rem(near_me + i, near_n))))
     crossed = ys * (ls - 1)
     if crossed:
@@ -160,49 +159,43 @@
     def clipped(values):
         return jnp.minimum(jnp.maximum(values, 0.0), box)
 
-    weighted = (signs_ref[...] * clipped(start_ref[...])).astype(BF16)
+    weighted_ref[0 : start_ref.shape[0], :] = (signs_ref[...] * clipped(start_ref[...])).astype(BF16)
     own_rows = pl.ds(pl.multiple_of(c * piece, 8), piece)
     signs_row = signs_ref[own_rows, :]
     dual = clipped(start_ref[own_rows, :])
     mult = jnp.zeros_like(dual)
+    zero = jnp.zeros((1, settings), F32)
 
     from_here = lax.div(g, ls) == y
     to_side = lax.rem(g, ls)
-    local = jnp.logical_and(g == c, lax.rem(spot, ls) == l)
 
     def first_copies(j, device):
         rows_j = pl.ds(pl.multiple_of(j * piece, 8), piece)
         return (
-            remote(start_ref.at[rows_j], first_ref, first_ss.at[0, lax.div(j, ls)], first_rs.at[0], device),
-            remote(labels_ref, first_labels_ref, first_ss.at[1, lax.div(j, ls)], first_rs.at[1], device),
+            remote(start_ref.at[rows_j], first_ref, first_ss.at[0], first_rs.at[0], device),
+            remote(labels_ref, first_labels_ref, first_ss.at[1 + lax.div(j, ls)], first_rs.at[1], device),
         )
 
-    def first_each(act):
+    def first_start():
         def one(i):
             j = i * ls + l
-            to = flip(j)
-
-            @pl.when(jnp.logical_not(jnp.logical_and(to == g, to_side == l)))
-            def _():
-                device = {"row_0": lax.div(to, xs), "row_1": lax.rem(to, xs), "col_1": to_side}
-                for copy in first_copies(j, device):
-                    act(copy)
+            for copy in first_copies(j, chip(flip(j)) | {"col_1": to_side}):
+                copy.start()
 
         @pl.when(from_here)
         def _():
             loop(0, groups // ls, one)
 
+    def first_sent():
+        @pl.when(from_here)
+        def _():
+            sent = start_ref.at[pl.ds(0, groups // ls * piece)]
+            remote(sent, sent, first_ss.at[0], first_rs.at[0], partner).wait_send()
+            loop(0, groups // ls, lambda i: first_copies(i * ls + l, partner)[1].wait_send())
+
     def first_arrived():
-        @pl.when(jnp.logical_not(local))
-        def _():
-            for copy in first_copies(0, partner):
-                copy.wait_recv()
-
-        @pl.when(local)
-        def _():
-            first_ref[...] = start_ref[pl.ds(pl.multiple_of(spot * piece, 8), piece), :]
-            first_labels_ref[...] = labels_ref[...]
-
+        for copy in first_copies(0, partner):
+            copy.wait_recv()
         write_signs(first_labels_ref, first_signs_ref)
         return clipped(first_ref[...]), first_signs_ref[pl.ds(pl.multiple_of(spot * piece, 8), piece), :]
 
@@ -289,7 +282,7 @@
         j = flip(i)
         return (
             remote(row_send.at[s, j], row_recv.at[s, g], row_ss.at[s], row_rs.at[s], chip(i)),
-            remote(rscale_send.at[s], rscale_recv.at[s, g], rscale_ss.at[s], rscale_rs.at[s], chip(i)),
+            remote(rscale_send.at[s, lax.div(i, xs)], rscale_recv.at[s, g], rscale_ss.at[s], rscale_rs.at[s], chip(i)),
         )
 
     def row_all(s):
@@ -299,28 +292,45 @@
             remote(rscale_recv.at[s, rest], rscale_recv.at[s, rest], rscale_ss.at[s], rscale_rs.at[s], partner),
         )
 
-    def core_copy(s):
-        return remote(part_ref.at[other], core_recv.at[s], core_ss.at[s], core_rs.at[s], partner)
-
-    def transposed_half(which, weighted):
-        columns = pl.ds(pl.multiple_of(which * half, 128) if half % 128 == 0 else which * half, half)
-        product = lax.dot_general(
-            kernel_ref[:, columns], weighted, (((0,), (0,)), ((), ())), preferred_element_type=F32
+    planes = sorted(range(hs), key=lambda d: -min(d, hs - d))
+
+    def core_copy(s, plane):
+        at = pl.ds(plane * xs, xs)
+        return remote(
+            part_ref.at[other, at], core_recv.at[s, at], core_ss.at[s, plane], core_rs.at[s, plane], partner
         )
-        part_ref[which] = product.reshape(part_ref.shape[1:])
+
+    def core_sent(s):
+        for plane in range(hs):
+            core_copy(s, plane).wait_send()
+
+    held = kernel_ref.shape[0]
+
+    def transposed_part(which, plane):
+        at = pl.multiple_of(which * half + plane * (xs * piece), 32)
+        product = jnp.dot(
+            turned_ref[pl.ds(at, xs * piece), :], weighted_ref[0:held, :], preferred_element_type=F32
+        )
+        part_ref[which, pl.ds(plane * xs, xs)] = product.reshape(xs, piece, settings)
         return jnp.sum(product, axis=0, keepdims=True)
 
-    def transposed_send(s):
-        core_copy(s).wait_recv()
-        both = part_ref[k] + core_recv[s]
-        part_ref[k] = both
-        row_send[s], rscale_send[s] = coded(both)
-
-        def send(i):
-            for copy in row_copies(s, lax.rem(g + i, groups)):
-                copy.start()
-
-        spread(groups, send)
+    def transposed_send(s, before):
+        for d in planes:
+            plane = lax.rem(h + d, hs)
+            before(d, plane)
+            core_copy(s, plane).wait_recv()
+            at = pl.ds(plane * xs, xs)
+            both = part_ref[k, at] + core_recv[s, at]
+            part_ref[k, at] = both
+            row_send[s, at], rscale_send[s, plane] = coded(both)
+
+            def send(i):
+                for copy in row_copies(s, plane * xs + lax.rem(x + i, xs)):
+                    copy.start()
+
+            spread(xs, send)
+            if d:
+                send(0)
 
     def transposed_sum(s):
         row_recv[s, g] = jnp.zeros(row_recv.shape[2:], I16)
@@ -329,67 +339,78 @@
             copy.wait_recv()
         return part_ref[k, spot] + decoded_sum(row_recv[s], rscale_recv[s])
 
-    zero = jnp.zeros((1, box.shape[1]), F32)
 
     load_k.wait()
-    far_sum = transposed_half(other, weighted)
-    pl.semaphore_wait(barrier, far_n - 1 + near_n - 1 + crossed)
-    core_copy(0).start()
-    product_sum = far_sum + transposed_half(k, weighted)
+    turned_ref[...] = jnp.transpose(kernel_ref[...])
+    product_sum = zero
+    for which in (other, k):
+        for plane in range(hs):
+            product_sum = product_sum + transposed_part(which, plane)
     ones = jnp.ones((8, kernel_ref.shape[0]), BF16)
     kcore_ref[k] = jnp.dot(ones, kernel_ref[...], preferred_element_type=F32)[0:1]
+    pl.semaphore_wait(barrier, far_n - 1 + near_n - 1 + crossed)
     sum_start(0, local_bias(dual, mult, signs_row, product_sum), zero)
+    for d in planes:
+        core_copy(0, lax.rem(h + d, hs)).start()
+    first_start()
     ksum_copy(kcore_ref, k, 0, partner).start()
-    transposed_send(0)
-    first_each(lambda copy: copy.start())
+    transposed_send(0, lambda d, plane: None)
     ksum_x()
     sum_middle(0)
     ksum_h()
     q_sum = transposed_sum(0)
-    core_copy(0).wait_send()
+    core_sent(0)
     dual, signs_col = first_arrived()
     mult = jnp.zeros_like(dual)
+    offset = sum_end(0)[0:1] / total
+    state, dual, mult, gap = update(signs_col * q_sum, dual, mult, signs_col, offset)
+
+    gat_ref[mine] = (signs_col * dual).astype(BF16)
+
+    def gat_copy(slot, send, recv, device):
+        return remote(gat_ref.at[slot], gat_ref.at[slot], send, gat_rs.at[recv], device)
+
+    spread(groups, lambda i: gat_copy(mine, gat_ss.at[0], spot, chip(lax.rem(g + i, groups))).start())
+    gat_copy(mine, fwd_ss.at[0], groups, partner).start()
     ksum_send[...] = ksum_row()
     ksum = ksum_of(ksum_send[...], mine)
-    offset = sum_end(0)[0:1] / total
-    state, dual, mult, gap = update(signs_col * q_sum, dual, mult, signs_col, offset)
-
-    gat_ref[mine] = (signs_col * dual).astype(BF16)
-
-    def gat_copy(slot, send, device):
-        return remote(gat_ref.at[slot], gat_ref.at[slot], send, gat_rs.at[slot], device)
-
-    spread(groups, lambda i: gat_copy(mine, gat_ss.at[0], chip(lax.rem(g + i, groups))).start())
-    gat_copy(mine, fwd_ss.at[0], partner).start()
     weighted = gat_ref[mine].astype(F32)
     sum_start(1, local_bias(dual, mult, signs_col, jnp.sum(ksum * weighted, axis=0, keepdims=True)), gap)
+    def forward(i):
+        at = flip(lax.rem(g + i, groups))
+        gat_copy(k * groups + at, fwd_ss.at[0], at, partner).wait_recv()
+        gat_copy(k * groups + at, fwd_ss.at[0], groups, partner).start()
+
+    loop(1, groups, forward)
+    sum_middle(1)
+    theirs = gat_ref.at[pl.ds(other * groups, groups)]
+    remote(theirs, theirs, fwd_ss.at[0], gat_rs.at[groups], partner).wait_recv()
     move_state(0, state, to_row)
     move_ksum = remote(ksum_send, ksum_recv, kmove_sem.at[0], kmove_sem.at[1], to_row)
     move_ksum.start()
-
-    def forward(i):
-        slot = k * groups + flip(lax.rem(g + i, groups))
-        gat_copy(slot, fwd_ss.at[0], partner).wait_recv()
-        gat_copy(slot, fwd_ss.at[0], partner).start()
-
-    loop(1, groups, forward)
-    sum_middle(1)
-    loop(0, groups, lambda i: gat_copy(other * groups + i, fwd_ss.at[0], partner).wait_recv())
-    gathered = gat_ref[...].astype(F32).reshape(rows * piece, -1).astype(BF16)
-    product = jnp.dot(kernel_ref[...], gathered, preferred_element_type=F32)
-    product = product.reshape(cols, piece, settings)
-    col_send[...], cscale_send[...] = coded(product)
-    part_ref[0] = product
-
-    def col_copies(i):
-        return (
-            remote(col_send.at[i], col_recv.at[c], col_ss.at[0], col_rs.at[0], column(i)),
-            remote(cscale_send, cscale_recv.at[c], cscale_ss.at[0], cscale_rs.at[0], column(i)),
-        )
+    weighted_ref[...] = gat_ref[...].astype(F32).reshape(rows * piece, -1).astype(BF16)
+    per = 2 * ls
+    quads = cols // per
 
     def col_start(i):
-        for copy in col_copies(lax.rem(c + i, cols)):
-            copy.start()
+        remote(col_send.at[i], col_recv.at[c], col_ss.at[0], col_rs.at[0], column(i)).start()
+        remote(
+            cscale_send.at[lax.div(i, per)], cscale_recv.at[c], cscale_ss.at[0], cscale_rs.at[0], column(i)
+        ).start()
+
+    for d in sorted(range(quads), key=lambda d: -min(d, quads - d)):
+        quad = lax.rem(lax.div(c, per) + d, quads)
+        at = pl.ds(quad * per, per)
+        product = jnp.dot(
+            kernel_ref[pl.ds(pl.multiple_of(quad * (per * piece), 32), per * piece), :], weighted_ref[...],
+            preferred_element_type=F32,
+        ).reshape(per, piece, settings)
+        part_ref[0, at] = product
+        col_send[at], cscale_send[quad] = coded(product)
+        if d:
+            loop(0, per, lambda i: col_start(quad * per + i))
+        else:
+            loop(1, per, lambda i: col_start(quad * per + lax.rem(lax.rem(c, per) + i, per)))
 
     rest = pl.ds(0, cols - 1)
     col_all = (
@@ -397,7 +418,6 @@
         remote(cscale_recv.at[rest], cscale_recv.at[rest], cscale_ss.at[0], cscale_rs.at[0], partner),
     )
 
-    spread(cols, col_start)
     col_recv[c] = jnp.zeros(col_recv.shape[1:], I16)
     cscale_recv[c] = jnp.zeros(cscale_recv.shape[1:], F32)
     for copy in col_all:
@@ -405,7 +425,7 @@
     q_sum = part_ref[0, c] + decoded_sum(col_recv[...], cscale_recv[...])
     dual, mult = arrived_state(0)
     sums = sum_end(1)
-    gaps_ref[0:1, :] = sums[1:2] / total
+    gaps_out[0:1, :] = sums[1:2] / total
     offset = sums[0:1] / total
     state, dual, mult, gap = update(signs_row * q_sum, dual, mult, signs_row, offset)
 
@@ -420,35 +440,34 @@
     weighted = pcol_ref[c].astype(F32)
     ksum = ksum_of(ksum_recv[...], lax.rem(block, rows))
     sum_start(2, local_bias(dual, mult, signs_row, jnp.sum(ksum * weighted, axis=0, keepdims=True)), gap)
+    pcol_all.wait_recv()
     move_state(1, state, to_column)
-    pcol_all.wait_recv()
-    weighted = pcol_ref[...].astype(F32).reshape(cols * piece, -1).astype(BF16)
-    transposed_half(other, weighted)
-    core_copy(1).start()
-    transposed_half(k, weighted)
+    weighted_ref[0:held, :] = pcol_ref[...].astype(F32).reshape(held, -1).astype(BF16)
+    for d in planes:
+        plane = lax.rem(h + d, hs)
+        transposed_part(other, plane)
+        core_copy(1, plane).start()
     sum_middle(2)
-    transposed_send(1)
+    transposed_send(1, lambda d, plane: transposed_part(k, plane))
     q_sum = transposed_sum(1)
     dual, mult = arrived_state(1)
     sums = sum_end(2)
-    gaps_ref[1:2, :] = sums[1:2] / total
+    gaps_out[1:2, :] = sums[1:2] / total
     offset = sums[0:1] / total
     state, dual, mult, gap = update(signs_col * q_sum, dual, mult, signs_col, offset)
 
     sum_start(3, zero, gap)
     move_state(2, state, to_row)
-    offset_ref[...] = offset
-    store_o = pltpu.make_async_copy(offset_ref, offset_out, store_sem.at[0])
-    store_o.start()
+    offset_out[...] = offset
     for t in range(3):
         near_all(t).wait_send()
         far_all(t).wait_send()
     state_copy(0, to_row).wait_send()
     state_copy(1, to_row).wait_send()
-    core_copy(1).wait_send()
+    core_sent(1)
     for copy in row_all(0) + row_all(1) + col_all:
         copy.wait_send()
-    first_each(lambda copy: copy.wait_send())
+    first_sent()
     rest = pl.ds(0, groups - 1)
     remote(gat_ref.at[rest], gat_ref.at[rest], gat_ss.at[0], gat_rs.at[0], partner).wait_send()
     rest = pl.ds(0, groups)
@@ -461,20 +480,10 @@
     ksum_all(kh_ref, 2).wait_send()
     sum_middle(3)
     state_copy(2, to_row).wait_send()
-    dual_ref[...], mult_ref[...] = arrived_state(2)
-    store_d = pltpu.make_async_copy(dual_ref, dual_out, store_sem.at[1])
-    store_m = pltpu.make_async_copy(mult_ref, mult_out, store_sem.at[2])
-    store_d.start()
-    store_m.start()
-    gaps_ref[2:3, :] = sum_end(3)[1:2] / total
-    store_g = pltpu.make_async_copy(gaps_ref, gaps_out, store_sem.at[3])
-    store_g.start()
+    dual_out[...], mult_out[...] = arrived_state(2)
+    gaps_out[2:3, :] = sum_end(3)[1:2] / total
     near_all(3).wait_send()
     far_all(3).wait_send()
-    store_o.wait()
-    store_d.wait()
-    store_m.wait()
-    store_g.wait()
 
 
 def hand_over(*refs):
@@ -495,18 +504,17 @@
     dma = pltpu.SemaphoreType.DMA
     vmem = pltpu.VMEM
     scratch = [
-        vmem((height, width), BF16), vmem((height // wide, wide), jnp.int32), vmem((height, settings), F32),
-        vmem((1, settings), F32), vmem((1, settings), F32), vmem((piece, settings), F32), vmem((piece, settings), F32),
-        vmem((ITERS, settings), F32), vmem((1, settings), F32), vmem((height, settings), F32),
-        vmem((ks, groups, piece, settings), F32), dma((5,)), dma((4,)),
-        vmem((piece, settings), F32), vmem((height // wide, wide), jnp.int32), vmem((height, settings), F32), dma((2, groups // ls)), dma((2,)),
+        vmem((height, width), BF16), vmem((width, height), BF16), vmem((width, settings), BF16), vmem((height // wide, wide), jnp.int32), vmem((height, settings), F32),
+        vmem((1, settings), F32), vmem((1, settings), F32), vmem((height, settings), F32),
+        vmem((ks, groups, piece, settings), F32), dma((5,)),
+        vmem((piece, settings), F32), vmem((height // wide, wide), jnp.int32), vmem((height, settings), F32), dma((1 + groups // ls,)), dma((2,)),
         vmem((3, piece, settings), F32), vmem((3, piece, settings), F32), dma((3,)), dma((3,)),
-        vmem((2, groups, piece, settings), F32), dma((2,)), dma((2,)),
+        vmem((2, groups, piece, settings), F32), dma((2, hs)), dma((2, hs)),
         vmem((2, groups, piece, settings), I16), vmem((2, groups, piece, settings), I16), dma((2,)), dma((2,)),
-        vmem((2, 1, settings), F32), vmem((2, groups, 1, settings), F32), dma((2,)), dma((2,)),
-        vmem((rows, piece, settings), BF16), dma((1,)), dma((rows,)), dma((1,)),
+        vmem((2, hs, 1, settings), F32), vmem((2, groups, 1, settings), F32), dma((2,)), dma((2,)),
+        vmem((rows, piece, settings), BF16), dma((1,)), dma((groups + 1,)), dma((1,)),
         vmem((cols, piece, settings), I16), vmem((cols, piece, settings), I16), dma((1,)), dma((1,)),
-        vmem((1, settings), F32), vmem((cols, 1, settings), F32), dma((1,)), dma((1,)),
+        vmem((cols // (2 * ls), 1, settings), F32), vmem((cols, 1, settings), F32), dma((1,)), dma((1,)),
         vmem((cols, piece, settings), BF16), dma((1,)), dma((1,)),
         vmem((4, near_n, 2, settings), F32), dma((4,)), dma((4,)),
         vmem((4, far_n, 2, settings), F32), dma((4,)), dma((4,)),
@@ -519,15 +527,17 @@
         jax.ShapeDtypeStruct(shape, F32)
         for shape in ((piece, settings), (piece, settings), (ITERS, settings), (1, settings))
     )
+    kept = tuple(vmem(shape.shape, F32) for shape in outs_shape)
     outs = pl.pallas_call(
         functools.partial(admm, dims, total),
-        out_shape=outs_shape,
+        out_shape=kept,
         in_specs=[in_hbm] * 5,
-        out_specs=(in_hbm,) * 4,
+        out_specs=(in_vmem,) * 4,
         scratch_shapes=scratch,
         compiler_params=pltpu.CompilerParams(collective_id=0, has_side_effects=True),
         name="admm",
     )(kernel, labels.reshape(height // wide, wide), start_dual, penalty[None, :], box[None, :])
+    outs = [pltpu.with_memory_space_constraint(out, vmem) for out in outs]
     dual, mult, gaps, offset = pl.pallas_call(
         hand_over, out_shape=outs_shape, in_specs=[in_vmem] * 4, out_specs=(in_vmem,) * 4, name="hand_over"
     )(*outs)

time: 78.3 us -> 74.6 us (0.953)
  Pallas kernels: 77.5 us -> 73.8 us
    pallas_call x1, Pallas kernels: 76.1 us -> 73.2 us  [body(): pl.pallas_call(functools.partial(admm, dims, total), out_shape=kept, in_s...]
where the time goes in v4:
time: 74.6 us; the launch traced here: 74.4 us
  Pallas kernels  73.8 us (99%)
    pallas_call x1, Pallas kernels, body(): pl.pallas_call(functools.partial(admm, dims, total), out_shape=kept, in_s...  73.2 us

profile of v4, /device:TPU:1, one launch (start us, length us, event | category | flops | bytes accessed | tf_op | source)
XLA Modules:
  0.0 74.4 jit_solution(11155976931614962588)
XLA Ops:
  0.6 73.2 %admm.1 = (f32[40,128]{1,0:T(8,128)S(1)}, f32[40,128]{1,0:T(8,128)S(1)}, f32[3,128]{1,0:T(4,128)S(1)}, f32[1,128]{1,0:T(1,128)S(1)}) custom-call(bf16[640,1280]{1,0:T(8,128)(2,1)} %kernel_hbm.1, s32[5,128]{1,0:T(8,128)} %bitcast.4, f32[640,128]{1,0:T(8,128)} %start_hbm.1, f32[1,128]{1,0:T(1,128)} %bitcast.5, f32[1,128]{1,0:T(1,128)} %bitcast.6), custom_call_target="tpu_custom_call" | custom-call | tf_op jit(solution)/shard_map/admm/pallas_call | solution.py:531
  73.8 0.6 hand_over.1

commit v5 on v4

--- a/solution.py
+++ b/solution.py
@@ -91,8 +91,8 @@
     piece, settings = state_send.shape[1:]
     half = groups * piece
     near_n, far_n = ys * ks, hs * xs * ls
-    near_me = k * ys + y
-    far_me = l * groups + g
+    near_me = y * ks + k
+    far_me = g * ls + l
     other = 1 - k
 
     def chip(to):
@@ -108,11 +108,11 @@
         }
 
     def near(to):
-        return {"row_2": lax.div(to, ys), "col_0": lax.rem(to, ys)}
+        return {"row_2": lax.rem(to, ks), "col_0": lax.div(to, ks)}
 
     def far(to):
-        on = lax.rem(to, groups)
-        return {"row_0": lax.div(on, xs), "row_1": lax.rem(on, xs), "col_1": lax.div(to, groups)}
+        on = lax.div(to, ls)
+        return {"row_0": lax.div(on, xs), "row_1": lax.rem(on, xs), "col_1": lax.rem(to, ls)}
 
     partner = {"row_2": other}
     spot = flip(g)
@@ -143,12 +143,6 @@
 
     spread(far_n, lambda i: greet(far(lax.rem(far_me + i, far_n))))
     loop(1, near_n, lambda i: greet(near(lax.rem(near_me + i, near_n))))
-    crossed = ys * (ls - 1)
-    if crossed:
-        def cross(i):
-            greet({"col_0": lax.rem(i, ys), "col_1": lax.rem(l + 1 + lax.div(i, ys), ls)})
-        loop(0, crossed, cross)
-
     load_l.wait()
     write_signs(labels_ref, signs_ref)
     load_b.wait()
@@ -348,7 +342,7 @@
             product_sum = product_sum + transposed_part(which, plane)
     ones = jnp.ones((8, kernel_ref.shape[0]), BF16)
     kcore_ref[k] = jnp.dot(ones, kernel_ref[...], preferred_element_type=F32)[0:1]
-    pl.semaphore_wait(barrier, far_n - 1 + near_n - 1 + crossed)
+    pl.semaphore_wait(barrier, far_n - 1 + near_n - 1)
     sum_start(0, local_bias(dual, mult, signs_row, product_sum), zero)
     for d in planes:
         core_copy(0, lax.rem(h + d, hs)).start()

time: 74.6 us -> 73.9 us (level)
  no operation moved by 1% of the time
where the time goes in v5:
time: 73.9 us; the launch traced here: 73.7 us
  Pallas kernels  73.1 us (99%)
    pallas_call x1, Pallas kernels, body(): pl.pallas_call(functools.partial(admm, dims, total), out_shape=kept, in_s...  72.4 us

profile of v5, /device:TPU:1, one launch (start us, length us, event | category | flops | bytes accessed | tf_op | source)
XLA Modules:
  0.0 73.7 jit_solution(10876890011352868093)
XLA Ops:
  0.6 72.4 %admm.1 = (f32[40,128]{1,0:T(8,128)S(1)}, f32[40,128]{1,0:T(8,128)S(1)}, f32[3,128]{1,0:T(4,128)S(1)}, f32[1,128]{1,0:T(1,128)S(1)}) custom-call(bf16[640,1280]{1,0:T(8,128)(2,1)} %kernel_hbm.1, s32[5,128]{1,0:T(8,128)} %bitcast.4, f32[640,128]{1,0:T(8,128)} %start_hbm.1, f32[1,128]{1,0:T(1,128)} %bitcast.5, f32[1,128]{1,0:T(1,128)} %bitcast.6), custom_call_target="tpu_custom_call" | custom-call | tf_op jit(solution)/shard_map/admm/pallas_call | solution.py:525
  73.1 0.6 hand_over.1
